TPU v7x, 32 devices: a whole 2x2x4 slice. The times are simulated.
32 devices in a mesh: row: 8 (over z, x), mem: 2 (over core), lev: 2 (over y).
Axes of the slice: x: 2, y: 2, z: 4, core: 2. Of those that a mesh axis runs over, the one named last changes fastest.
Arguments:
- control_fields: bfloat16 [4, 6, 256, 2048], P('mem', 'lev', 'row'), may hold values from -6 to 6
- perturbations: bfloat16 [3, 4, 6, 256, 2048], P(None, 'mem', 'lev', 'row'), may hold values from -3 to 3
- column_taper: bfloat16 [2048, 2048], P('row'), may hold values from -1 to 2, as said below
- row_taper: bfloat16 [256, 256], P('row'), may hold values from -1 to 2, as said below
- courant_numbers: float32 [3, 6, 256, 2048], P(None, 'lev', 'row', 'mem'), may hold values from -0.3 to 0.3
- tracer_slope: float32 [2, 6, 256, 2048], P(None, 'lev', 'row', 'mem'), may hold values from -3 to 3
Outputs:
- increment: float32 [3, 6, 256, 2048], P(None, 'lev', 'row', 'mem')
Inputs may be any that keep to these rules, and one draw needn't show every extreme that they name: `column_taper`: A square matrix. `row_taper`: A square matrix.
All inputs are finite; a program needn't handle non-finite values.
Results may differ from a plain program's by a relative error of at most 0.0048.
Values may be sent and summed in bfloat16 or wider, within the bound.
A program may use at most 64 MiB of HBM per device.

v0:
```python
import jax
import jax.numpy as jnp
from jax import lax
from jax.sharding import PartitionSpec as P

STEPS = 4


def extended(block, sides, width):
    for axis, dim in sides:
        count = lax.axis_size(axis)
        forward = [(i, i + 1) for i in range(count - 1)]
        backward = [(target, source) for source, target in forward]
        low = lax.ppermute(
            lax.slice_in_dim(block, block.shape[dim] - width, None, axis=dim), axis, forward
        )
        high = lax.ppermute(lax.slice_in_dim(block, 0, width, axis=dim), axis, backward)
        block = jnp.concatenate([low, block, high], axis=dim)
    return block


def upwind(middle, behind, forward, velocity):
    return jnp.maximum(velocity, 0.0) * (middle - behind) + jnp.minimum(velocity, 0.0) * (
        forward - middle
    )


def advance(present, courant_numbers, tracer_slope, padded):
    middle = padded[:, 1:-1, 1:-1, 1:-1]
    change = upwind(
        middle, padded[:, :-2, 1:-1, 1:-1], padded[:, 2:, 1:-1, 1:-1], courant_numbers[0]
    )
    change = change + upwind(
        middle, padded[:, 1:-1, :-2, 1:-1], padded[:, 1:-1, 2:, 1:-1], courant_numbers[1]
    )
    change = change + upwind(
        middle, padded[:, 1:-1, 1:-1, :-2], padded[:, 1:-1, 1:-1, 2:], courant_numbers[2]
    )
    shifted = present - change
    source = present[0] * tracer_slope[0] + present[1] * tracer_slope[1]
    return jnp.concatenate([shifted[:2], shifted[2:] - source[None]], axis=0)


def on_device(
    control_fields, perturbations, column_taper, row_taper, courant_numbers, tracer_slope
):
    member_count, level_count, row_count, column_count = control_fields.shape
    field_count = member_count * level_count
    flattened = control_fields.reshape(field_count * row_count, column_count)
    block_width = column_count // lax.axis_size("mem")
    own_block = lax.dynamic_slice_in_dim(
        column_taper, lax.axis_index("mem") * block_width, block_width, 1
    )
    column_block = lax.all_gather(own_block, "row", axis=0, tiled=True)
    first_pass = jnp.dot(
        flattened,
        lax.all_gather(column_block, "mem", axis=1, tiled=True),
        preferred_element_type=jnp.float32,
    )
    first_pass = first_pass.astype(jnp.bfloat16).reshape(field_count, row_count, column_count)
    row_whole = lax.all_gather(row_taper, "row", axis=0, tiled=True)
    tapered = jnp.einsum(
        "ij,fjc->fic",
        row_whole,
        lax.all_to_all(first_pass, "row", split_axis=2, concat_axis=1, tiled=True),
        preferred_element_type=jnp.float32,
    )
    localized = lax.all_to_all(
        tapered.astype(jnp.bfloat16), "row", split_axis=1, concat_axis=2, tiled=True
    )
    localized = localized.reshape(member_count, level_count, row_count, column_count)
    weighted = jnp.einsum(
        "kmlrc,mlrc->klrc", perturbations, localized, preferred_element_type=jnp.float32
    )
    summed = lax.psum(weighted, "mem")
    own_columns = column_count // lax.axis_size("mem")
    margin = STEPS
    widened = jnp.pad(summed, ((0, 0), (0, 0), (0, 0), (margin, margin)))
    present = lax.dynamic_slice_in_dim(
        widened, lax.axis_index("mem") * own_columns, own_columns + 2 * margin, 3
    )
    background = jnp.concatenate([courant_numbers, tracer_slope], axis=0)
    background = extended(background, (("mem", 3),), margin - 1)
    background = jnp.pad(background, ((0, 0), (0, 0), (0, 0), (1, 1)))
    courant_near = background[:3]
    slope_near = background[3:]
    for advect_step in range(STEPS):
        padded = extended(present, (("row", 2), ("lev", 1)), 1)
        padded = jnp.pad(padded, ((0, 0), (0, 0), (0, 0), (1, 1)))
        present = advance(present, courant_near, slope_near, padded)
    return present[:, :, :, margin : margin + own_columns]


def solution(mesh):
    placed = (
        P("mem", "lev", "row", None),
        P(None, "mem", "lev", "row", None),
        P("row", None),
        P("row", None),
        P(None, "lev", "row", "mem"),
        P(None, "lev", "row", "mem"),
    )
    return jax.shard_map(
        on_device,
        mesh=mesh,
        in_specs=placed,
        out_specs=P(None, "lev", "row", "mem"),
        check_vma=False,
    )
```

profile of v0, /device:TPU:0, one launch (start us, length us, event | category | flops | bytes accessed | tf_op | source)
XLA Modules:
  0.0 356.1 jit_solution(13105754108425344147)
XLA Ops:
  8.7 76.3 %all-gather.3.cloned.1.call-done = bf16[2048,1024]{1,0:T(8,128)(2,1)} async-done(((bf16[256,1024]{1,0:T(8,128)(2,1)}), bf16[2048,1024]{1,0:T(8,128)(2,1)}) %all-gather.3.cloned.1.call-update) | async-done | bytes 4194320 | tf_op jit(solution)/shard_map/all_gather | solution.py:54
  85.0 19.9 %all-gather.5.cloned.1.call-done = bf16[2048,2048]{1,0:T(8,128)(2,1)} async-done(((bf16[2048,1024]{1,0:T(8,128)(2,1)}), bf16[2048,2048]{1,0:T(8,128)(2,1)}) %all-gather.5.cloned.1.call-update) | async-done | bytes 8388624 | tf_op jit(solution)/shard_map/all_gather | solution.py:57
  105.0 5.2 %convolution_convert_fusion = bf16[2048,192]{0,1:T(8,128)(2,1)S(1)} fusion(bf16[192,2048]{1,0:T(8,128)(2,1)S(1)} %bitcast.47, bf16[2048,2048]{1,0:T(8,128)(2,1)} %all-gather.5.cloned.1.call-done), kind=kOutput, calls=%fused_computation.23 | convolution fusion | flops 1611005952 | bytes 9961472 | tf_op jit(solution)/shard_map/dot_general | solution.py:55
  110.2 4.2 %copy.15 = bf16[6,32,2048]{1,0,2:T(8,128)(2,1)} copy(bf16[6,32,2048]{2,1,0:T(8,128)(2,1)S(1)} %bitcast.46) | data formatting | bytes 1572864 | tf_op jit(solution)/shard_map/reshape | solution.py:60
  114.3 5.7 %reshape.16 = bf16[8,2,24576]{2,1,0:T(2,128)(2,1)} reshape(bf16[2048,6,32]{2,1,0:T(8,128)(2,1)} %bitcast.41) | data formatting | bytes 1572864
  120.0 5.9 %all-to-all-start = ((bf16[8,2,24576]{2,1,0:T(2,128)(2,1)}), bf16[8,2,24576]{2,1,0:T(2,128)(2,1)S(1)}, u32[]{:S(2)}, u32[]{:S(2)}) async-start(bf16[8,2,24576]{2,1,0:T(2,128)(2,1)} %reshape.16), calls=%async_computation | async-start | bytes 1572864 | tf_op jit(solution)/shard_map/all_to_all | solution.py:65
  126.0 41.8 %all_gather.11 = bf16[256,256]{1,0:T(8,128)(2,1)S(1)} all-gather(bf16[32,256]{1,0:T(8,128)(2,1)S(1)} %copy-done.9), channel_id=1, replica_groups=mesh['row'=8,'mem'=2,'lev'=2] {'row'}, dimensions={0}, use_global_device_ids=true | all-gather | bytes 147456 | tf_op jit(solution)/shard_map/all_gather | solution.py:61
  167.8 4.1 %reshape.17 = bf16[2048,6,32]{2,1,0:T(8,128)(2,1)} reshape(bf16[8,2,24576]{2,1,0:T(2,128)(2,1)S(1)} %all-to-all-done) | data formatting | bytes 1572864
  171.9 4.1 %copy.17 = bf16[6,8,32,256]{3,2,1,0:T(8,128)(2,1)S(1)} copy(bf16[6,8,32,256]{2,0,3,1:T(8,128)(2,1)} %bitcast.42) | data formatting | bytes 1572864 | tf_op jit(solution)/shard_map/all_to_all | solution.py:65
  177.4 22.4 %all_to_all.33 = bf16[6,256,256]{2,0,1:T(8,128)(2,1)S(1)} all-to-all(bf16[6,256,256]{2,0,1:T(8,128)(2,1)S(1)} %copy.19), channel_id=1, replica_groups=mesh['row'=8,'mem'=2,'lev'=2] {'row'}, dimensions={1} | all-to-all | bytes 1572864 | tf_op jit(solution)/shard_map/all_to_all | solution.py:68
  205.9 19.7 %all-reduce.8.cloned.1.call-done = f32[3,3,32,2048]{3,2,1,0:T(8,128)} async-done(((f32[3,3,32,2048]{3,2,1,0:T(8,128)}), f32[3,3,32,2048]{3,2,1,0:T(8,128)}) %all-reduce.8.cloned.1.call-update) | async-done | bytes 2359312 | tf_op jit(solution)/shard_map/psum | solution.py:75
  227.1 3.6 %collective-permute-start.2 = (f32[3,3,1,1032]{3,2,1,0:T(1,128)S(1)}, f32[3,3,1,1032]{3,2,1,0:T(1,128)S(1)}, u32[]{:S(2)}, u32[]{:S(2)}) collective-permute-start(f32[3,3,1,1032]{3,2,1,0:T(1,128)S(1)} %get-tuple-element.5), channel_id=1, source_target_pairs={{0,4},{4,8},{8,12},{12,16},{16,20},{20,24},{24,28},{1,5},{5,9},{9,... | collective-permute-start | bytes 111464 | tf_op jit(solution)/shard_map/ppermute | solution.py:14
  232.5 4.2 %collective-permute-done.3 = f32[3,3,1,1032]{3,2,1,0:T(1,128)S(1)} collective-permute-done((f32[3,3,1,1032]{3,2,1,0:T(1,128)S(1)}, f32[3,3,1,1032]{3,2,1,0:T(1,128)S(1)}, u32[]{:S(2)}, u32[]{:S(2)}) %collective-permute-start.3) | collective-permute-done | bytes 37184 | tf_op jit(solution)/shard_map/ppermute | solution.py:17
  237.8 4.2 %collective-permute-start.4 = (f32[3,1,34,1032]{3,2,1,0:T(8,128)}, f32[3,1,34,1032]{3,2,1,0:T(8,128)}, u32[]{:S(2)}, u32[]{:S(2)}) collective-permute-start(f32[3,1,34,1032]{3,2,1,0:T(8,128)} %get-tuple-element.21), channel_id=1, source_target_pairs={{0,1},{2,3},{4,5},{6,7},{8,9},{10,11},{12,13},{14,15},{16,17},{18,... | collective-permute-start | bytes 1263176 | tf_op jit(solution)/shard_map/ppermute | solution.py:14
  248.1 3.0 concatenate.91
  252.3 4.9 %collective-permute-done.5 = f32[3,1,34,1032]{3,2,1,0:T(8,128)} collective-permute-done((f32[3,1,34,1032]{3,2,1,0:T(8,128)}, f32[3,1,34,1032]{3,2,1,0:T(8,128)}, u32[]{:S(2)}, u32[]{:S(2)}) %collective-permute-start.5) | collective-permute-done | bytes 421088 | tf_op jit(solution)/shard_map/ppermute | solution.py:17
  259.4 3.9 %fusion.52 = f32[3,3,32,1032]{3,2,1,0:T(8,128)S(1)} fusion(f32[3,3,32,1032]{3,2,1,0:T(8,128)S(1)} %copy-done.5, f32[3,5,34,1034]{3,2,1,0:T(8,128)S(1)} %select_maximum_fusion.15, f32[3,3,1,1032]{3,2,1,0:T(1,128)S(1)} %collective-permute-done.3, f32[3,3,1,1032]{3,2,1,0:T(1,128)S(1)} %collective-permute-done.2, f32[3,1,34,1032]{3,2,1,0:T(8,128)} %collective-permute-done.5, ...), kind=kLoop, calls=%fused_computation.144 | loop fusion | flops 7727616 | bytes 8049600 | tf_op jit(solution)/shard_map/sub | solution.py:39
  263.9 4.3 %collective-permute-start.6 = (f32[3,3,1,1032]{3,2,1,0:T(1,128)S(1)}, f32[3,3,1,1032]{3,2,1,0:T(1,128)S(1)}, u32[]{:S(2)}, u32[]{:S(2)}) collective-permute-start(f32[3,3,1,1032]{3,2,1,0:T(1,128)S(1)} %get-tuple-element.27), channel_id=1, source_target_pairs={{0,4},{4,8},{8,12},{12,16},{16,20},{20,24},{24,28},{1,5},{5,9},{9,... | collective-permute-start | bytes 111464 | tf_op jit(solution)/shard_map/ppermute | solution.py:14
  270.0 4.1 %collective-permute-done.7 = f32[3,3,1,1032]{3,2,1,0:T(1,128)S(1)} collective-permute-done((f32[3,3,1,1032]{3,2,1,0:T(1,128)S(1)}, f32[3,3,1,1032]{3,2,1,0:T(1,128)S(1)}, u32[]{:S(2)}, u32[]{:S(2)}) %collective-permute-start.7) | collective-permute-done | bytes 37184 | tf_op jit(solution)/shard_map/ppermute | solution.py:17
  277.1 8.5 %collective-permute-done.8 = f32[3,1,34,1032]{3,2,1,0:T(8,128)S(1)} collective-permute-done((f32[3,1,34,1032]{3,2,1,0:T(8,128)S(1)}, f32[3,1,34,1032]{3,2,1,0:T(8,128)S(1)}, u32[]{:S(2)}, u32[]{:S(2)}) %collective-permute-start.8) | collective-permute-done | bytes 421088 | tf_op jit(solution)/shard_map/ppermute | solution.py:14
  285.6 4.1 %collective-permute-done.9 = f32[3,1,34,1032]{3,2,1,0:T(8,128)S(1)} collective-permute-done((f32[3,1,34,1032]{3,2,1,0:T(8,128)S(1)}, f32[3,1,34,1032]{3,2,1,0:T(8,128)S(1)}, u32[]{:S(2)}, u32[]{:S(2)}) %collective-permute-start.9) | collective-permute-done | bytes 421088 | tf_op jit(solution)/shard_map/ppermute | solution.py:17
  290.7 2.8 fusion.36
  294.0 3.4 collective-permute-start.10
  299.2 4.1 %collective-permute-done.11 = f32[3,3,1,1032]{3,2,1,0:T(1,128)S(1)} collective-permute-done((f32[3,3,1,1032]{3,2,1,0:T(1,128)S(1)}, f32[3,3,1,1032]{3,2,1,0:T(1,128)S(1)}, u32[]{:S(2)}, u32[]{:S(2)}) %collective-permute-start.11) | collective-permute-done | bytes 37184 | tf_op jit(solution)/shard_map/ppermute | solution.py:17
  306.2 6.1 %collective-permute-done.12 = f32[3,1,34,1032]{3,2,1,0:T(8,128)S(1)} collective-permute-done((f32[3,1,34,1032]{3,2,1,0:T(8,128)S(1)}, f32[3,1,34,1032]{3,2,1,0:T(8,128)S(1)}, u32[]{:S(2)}, u32[]{:S(2)}) %collective-permute-start.12) | collective-permute-done | bytes 421088 | tf_op jit(solution)/shard_map/ppermute | solution.py:14
  312.3 4.1 %collective-permute-done.13 = f32[3,1,34,1032]{3,2,1,0:T(8,128)S(1)} collective-permute-done((f32[3,1,34,1032]{3,2,1,0:T(8,128)S(1)}, f32[3,1,34,1032]{3,2,1,0:T(8,128)S(1)}, u32[]{:S(2)}, u32[]{:S(2)}) %collective-permute-start.13) | collective-permute-done | bytes 421088 | tf_op jit(solution)/shard_map/ppermute | solution.py:17
  317.4 2.8 fusion.20
  320.7 4.3 %collective-permute-start.14 = (f32[3,3,1,1032]{3,2,1,0:T(1,128)S(1)}, f32[3,3,1,1032]{3,2,1,0:T(1,128)S(1)}, u32[]{:S(2)}, u32[]{:S(2)}) collective-permute-start(f32[3,3,1,1032]{3,2,1,0:T(1,128)S(1)} %get-tuple-element.23), channel_id=1, source_target_pairs={{0,4},{4,8},{8,12},{12,16},{16,20},{20,24},{24,28},{1,5},{5,9},{9,... | collective-permute-start | bytes 111464 | tf_op jit(solution)/shard_map/ppermute | solution.py:14
  326.7 4.2 %collective-permute-done.15 = f32[3,3,1,1032]{3,2,1,0:T(1,128)S(1)} collective-permute-done((f32[3,3,1,1032]{3,2,1,0:T(1,128)S(1)}, f32[3,3,1,1032]{3,2,1,0:T(1,128)S(1)}, u32[]{:S(2)}, u32[]{:S(2)}) %collective-permute-start.15) | collective-permute-done | bytes 37184 | tf_op jit(solution)/shard_map/ppermute | solution.py:17
  334.1 5.4 %collective-permute-done.16 = f32[3,1,34,1032]{3,2,1,0:T(8,128)S(1)} collective-permute-done((f32[3,1,34,1032]{3,2,1,0:T(8,128)S(1)}, f32[3,1,34,1032]{3,2,1,0:T(8,128)S(1)}, u32[]{:S(2)}, u32[]{:S(2)}) %collective-permute-start.16) | collective-permute-done | bytes 421088 | tf_op jit(solution)/shard_map/ppermute | solution.py:14
  339.5 4.4 %collective-permute-done.17 = f32[3,1,34,1032]{3,2,1,0:T(8,128)S(1)} collective-permute-done((f32[3,1,34,1032]{3,2,1,0:T(8,128)S(1)}, f32[3,1,34,1032]{3,2,1,0:T(8,128)S(1)}, u32[]{:S(2)}, u32[]{:S(2)}) %collective-permute-start.17) | collective-permute-done | bytes 421088 | tf_op jit(solution)/shard_map/ppermute | solution.py:17
  345.0 2.8 fusion.4
  (82 shorter events, 43.8 us)
Async XLA Ops:
  6.5 78.5 %all-gather.3.cloned.1.call-start = ((), (), s32[]{:S(2)}) async-start(), calls=%async_computation.2 | async-start | bytes 4718592 | tf_op jit(solution)/shard_map/all_gather | solution.py:54
  8.6 96.3 %all-gather.5.cloned.1.call-start = ((), (), s32[]{:S(2)}) async-start(), calls=%async_computation.3 | async-start | bytes 12582912 | tf_op jit(solution)/shard_map/all_gather | solution.py:57
  85.0 20.0 %copy-start.10 = (bf16[2,3,32,2048]{3,2,1,0:T(8,128)(2,1)S(1)}, bf16[2,3,32,2048]{3,2,1,0:T(8,128)(2,1)}, u32[]{:S(2)}) copy-start(bf16[2,3,32,2048]{3,2,1,0:T(8,128)(2,1)} %param.6) | copy-start | bytes 2359300
  120.0 6.0 %copy-start.9 = (bf16[32,256]{1,0:T(8,128)(2,1)S(1)}, bf16[32,256]{1,0:T(8,128)(2,1)}, u32[]{:S(2)}) copy-start(bf16[32,256]{1,0:T(8,128)(2,1)} %param.9) | copy-start | bytes 49156
  120.0 47.8 %all-to-all-start = ((bf16[8,2,24576]{2,1,0:T(2,128)(2,1)}), bf16[8,2,24576]{2,1,0:T(2,128)(2,1)S(1)}, u32[]{:S(2)}, u32[]{:S(2)}) async-start(bf16[8,2,24576]{2,1,0:T(2,128)(2,1)} %reshape.16), calls=%async_computation | async-start | bytes 1572864 | tf_op jit(solution)/shard_map/all_to_all | solution.py:65
  125.9 99.7 %all-reduce.8.cloned.1.call-start = ((), (), s32[]{:S(2)}) async-start(), calls=%async_computation.4 | async-start | bytes 4718592 | tf_op jit(solution)/shard_map/psum | solution.py:75
  200.6 1.7 copy-start.7
  204.3 1.5 copy-start.8
  205.9 37.4 %copy-start.6 = (f32[5,3,32,1024]{3,2,1,0:T(8,128)}, f32[5,3,32,1024]{3,2,1,0:T(8,128)S(1)}, u32[]{:S(2)}) copy-start(f32[5,3,32,1024]{3,2,1,0:T(8,128)S(1)} %constant_dynamic-update-slice_fusion) | copy-start | bytes 5898244
  225.6 6.5 %copy-start.2 = (f32[3,3,32,2048]{3,2,1,0:T(8,128)S(1)}, f32[3,3,32,2048]{3,2,1,0:T(8,128)}, u32[]{:S(2)}) copy-start(f32[3,3,32,2048]{3,2,1,0:T(8,128)} %all-reduce.8.cloned.1.call-done) | copy-start | bytes 7077892
  227.1 5.4 %collective-permute-start.2 = (f32[3,3,1,1032]{3,2,1,0:T(1,128)S(1)}, f32[3,3,1,1032]{3,2,1,0:T(1,128)S(1)}, u32[]{:S(2)}, u32[]{:S(2)}) collective-permute-start(f32[3,3,1,1032]{3,2,1,0:T(1,128)S(1)} %get-tuple-element.5), channel_id=1, source_target_pairs={{0,4},{4,8},{8,12},{12,16},{16,20},{20,24},{24,28},{1,5},{5,9},{9,... | collective-permute-start | bytes 111464 | tf_op jit(solution)/shard_map/ppermute | solution.py:14
  230.7 5.9 %collective-permute-start.3 = (f32[3,3,1,1032]{3,2,1,0:T(1,128)S(1)}, f32[3,3,1,1032]{3,2,1,0:T(1,128)S(1)}, u32[]{:S(2)}, u32[]{:S(2)}) collective-permute-start(f32[3,3,1,1032]{3,2,1,0:T(1,128)S(1)} %get-tuple-element.6), channel_id=1, source_target_pairs={{4,0},{8,4},{12,8},{16,12},{20,16},{24,20},{28,24},{5,1},{9,5},{13... | collective-permute-start | bytes 111464 | tf_op jit(solution)/shard_map/ppermute | solution.py:17
  232.5 10.9 %copy-start.4 = (f32[3,3,32,1032]{3,2,1,0:T(8,128)}, f32[3,3,32,1032]{3,2,1,0:T(8,128)S(1)}, u32[]{:S(2)}) copy-start(f32[3,3,32,1032]{3,2,1,0:T(8,128)S(1)} %pad_dynamic-slice_fusion.4) | copy-start | bytes 3566596
  237.8 14.5 %collective-permute-start.4 = (f32[3,1,34,1032]{3,2,1,0:T(8,128)}, f32[3,1,34,1032]{3,2,1,0:T(8,128)}, u32[]{:S(2)}, u32[]{:S(2)}) collective-permute-start(f32[3,1,34,1032]{3,2,1,0:T(8,128)} %get-tuple-element.21), channel_id=1, source_target_pairs={{0,1},{2,3},{4,5},{6,7},{8,9},{10,11},{12,13},{14,15},{16,17},{18,... | collective-permute-start | bytes 1263176 | tf_op jit(solution)/shard_map/ppermute | solution.py:14
  241.9 15.2 %collective-permute-start.5 = (f32[3,1,34,1032]{3,2,1,0:T(8,128)}, f32[3,1,34,1032]{3,2,1,0:T(8,128)}, u32[]{:S(2)}, u32[]{:S(2)}) collective-permute-start(f32[3,1,34,1032]{3,2,1,0:T(8,128)} %get-tuple-element.22), channel_id=1, source_target_pairs={{1,0},{3,2},{5,4},{7,6},{9,8},{11,10},{13,12},{15,14},{17,16},{19,... | collective-permute-start | bytes 1263176 | tf_op jit(solution)/shard_map/ppermute | solution.py:17
  243.4 2.8 collective-permute-start
  244.7 3.4 collective-permute-start.1
  251.1 6.0 %copy-start.5 = (f32[3,3,32,1032]{3,2,1,0:T(8,128)S(1)}, f32[3,3,32,1032]{3,2,1,0:T(8,128)}, u32[]{:S(2)}) copy-start(f32[3,3,32,1032]{3,2,1,0:T(8,128)} %copy-done.4) | copy-start | bytes 3566596
  259.3 3.9 %copy-start.3 = (f32[3,3,32,2048]{3,2,1,0:T(8,128)S(1)}, f32[3,3,32,2048]{3,2,1,0:T(8,128)}, u32[]{:S(2)}) copy-start(f32[3,3,32,2048]{3,2,1,0:T(8,128)} %all-reduce.8.cloned.1.call-done) | copy-start | bytes 7077892
  263.9 6.1 %collective-permute-start.6 = (f32[3,3,1,1032]{3,2,1,0:T(1,128)S(1)}, f32[3,3,1,1032]{3,2,1,0:T(1,128)S(1)}, u32[]{:S(2)}, u32[]{:S(2)}) collective-permute-start(f32[3,3,1,1032]{3,2,1,0:T(1,128)S(1)} %get-tuple-element.27), channel_id=1, source_target_pairs={{0,4},{4,8},{8,12},{12,16},{16,20},{20,24},{24,28},{1,5},{5,9},{9,... | collective-permute-start | bytes 111464 | tf_op jit(solution)/shard_map/ppermute | solution.py:14
  268.2 5.9 %collective-permute-start.7 = (f32[3,3,1,1032]{3,2,1,0:T(1,128)S(1)}, f32[3,3,1,1032]{3,2,1,0:T(1,128)S(1)}, u32[]{:S(2)}, u32[]{:S(2)}) collective-permute-start(f32[3,3,1,1032]{3,2,1,0:T(1,128)S(1)} %get-tuple-element.28), channel_id=1, source_target_pairs={{4,0},{8,4},{12,8},{16,12},{20,16},{24,20},{28,24},{5,1},{9,5},{13... | collective-permute-start | bytes 111464 | tf_op jit(solution)/shard_map/ppermute | solution.py:17
  274.3 11.3 %collective-permute-start.8 = (f32[3,1,34,1032]{3,2,1,0:T(8,128)S(1)}, f32[3,1,34,1032]{3,2,1,0:T(8,128)S(1)}, u32[]{:S(2)}, u32[]{:S(2)}) collective-permute-start(f32[3,1,34,1032]{3,2,1,0:T(8,128)S(1)} %get-tuple-element.19), channel_id=1, source_target_pairs={{0,1},{2,3},{4,5},{6,7},{8,9},{10,11},{12,13},{14,15},{16,17},{18,... | collective-permute-start | bytes 1263176 | tf_op jit(solution)/shard_map/ppermute | solution.py:14
  275.8 14.0 %collective-permute-start.9 = (f32[3,1,34,1032]{3,2,1,0:T(8,128)S(1)}, f32[3,1,34,1032]{3,2,1,0:T(8,128)S(1)}, u32[]{:S(2)}, u32[]{:S(2)}) collective-permute-start(f32[3,1,34,1032]{3,2,1,0:T(8,128)S(1)} %get-tuple-element.20), channel_id=1, source_target_pairs={{1,0},{3,2},{5,4},{7,6},{9,8},{11,10},{13,12},{15,14},{17,16},{19,... | collective-permute-start | bytes 1263176 | tf_op jit(solution)/shard_map/ppermute | solution.py:17
  294.0 5.2 %collective-permute-start.10 = (f32[3,3,1,1032]{3,2,1,0:T(1,128)S(1)}, f32[3,3,1,1032]{3,2,1,0:T(1,128)S(1)}, u32[]{:S(2)}, u32[]{:S(2)}) collective-permute-start(f32[3,3,1,1032]{3,2,1,0:T(1,128)S(1)} %get-tuple-element.25), channel_id=1, source_target_pairs={{0,4},{4,8},{8,12},{12,16},{16,20},{20,24},{24,28},{1,5},{5,9},{9,... | collective-permute-start | bytes 111464 | tf_op jit(solution)/shard_map/ppermute | solution.py:14
  297.4 5.9 %collective-permute-start.11 = (f32[3,3,1,1032]{3,2,1,0:T(1,128)S(1)}, f32[3,3,1,1032]{3,2,1,0:T(1,128)S(1)}, u32[]{:S(2)}, u32[]{:S(2)}) collective-permute-start(f32[3,3,1,1032]{3,2,1,0:T(1,128)S(1)} %get-tuple-element.26), channel_id=1, source_target_pairs={{4,0},{8,4},{12,8},{16,12},{20,16},{24,20},{28,24},{5,1},{9,5},{13... | collective-permute-start | bytes 111464 | tf_op jit(solution)/shard_map/ppermute | solution.py:17
  303.4 8.9 %collective-permute-start.12 = (f32[3,1,34,1032]{3,2,1,0:T(8,128)S(1)}, f32[3,1,34,1032]{3,2,1,0:T(8,128)S(1)}, u32[]{:S(2)}, u32[]{:S(2)}) collective-permute-start(f32[3,1,34,1032]{3,2,1,0:T(8,128)S(1)} %get-tuple-element.17), channel_id=1, source_target_pairs={{0,1},{2,3},{4,5},{6,7},{8,9},{10,11},{12,13},{14,15},{16,17},{18,... | collective-permute-start | bytes 1263176 | tf_op jit(solution)/shard_map/ppermute | solution.py:14
  304.9 11.5 %collective-permute-start.13 = (f32[3,1,34,1032]{3,2,1,0:T(8,128)S(1)}, f32[3,1,34,1032]{3,2,1,0:T(8,128)S(1)}, u32[]{:S(2)}, u32[]{:S(2)}) collective-permute-start(f32[3,1,34,1032]{3,2,1,0:T(8,128)S(1)} %get-tuple-element.18), channel_id=1, source_target_pairs={{1,0},{3,2},{5,4},{7,6},{9,8},{11,10},{13,12},{15,14},{17,16},{19,... | collective-permute-start | bytes 1263176 | tf_op jit(solution)/shard_map/ppermute | solution.py:17
  320.7 6.0 %collective-permute-start.14 = (f32[3,3,1,1032]{3,2,1,0:T(1,128)S(1)}, f32[3,3,1,1032]{3,2,1,0:T(1,128)S(1)}, u32[]{:S(2)}, u32[]{:S(2)}) collective-permute-start(f32[3,3,1,1032]{3,2,1,0:T(1,128)S(1)} %get-tuple-element.23), channel_id=1, source_target_pairs={{0,4},{4,8},{8,12},{12,16},{16,20},{20,24},{24,28},{1,5},{5,9},{9,... | collective-permute-start | bytes 111464 | tf_op jit(solution)/shard_map/ppermute | solution.py:14
  325.1 5.9 %collective-permute-start.15 = (f32[3,3,1,1032]{3,2,1,0:T(1,128)S(1)}, f32[3,3,1,1032]{3,2,1,0:T(1,128)S(1)}, u32[]{:S(2)}, u32[]{:S(2)}) collective-permute-start(f32[3,3,1,1032]{3,2,1,0:T(1,128)S(1)} %get-tuple-element.24), channel_id=1, source_target_pairs={{4,0},{8,4},{12,8},{16,12},{20,16},{24,20},{28,24},{5,1},{9,5},{13... | collective-permute-start | bytes 111464 | tf_op jit(solution)/shard_map/ppermute | solution.py:17
  331.1 8.4 %collective-permute-start.16 = (f32[3,1,34,1032]{3,2,1,0:T(8,128)S(1)}, f32[3,1,34,1032]{3,2,1,0:T(8,128)S(1)}, u32[]{:S(2)}, u32[]{:S(2)}) collective-permute-start(f32[3,1,34,1032]{3,2,1,0:T(8,128)S(1)} %get-tuple-element.15), channel_id=1, source_target_pairs={{0,1},{2,3},{4,5},{6,7},{8,9},{10,11},{12,13},{14,15},{16,17},{18,... | collective-permute-start | bytes 1263176 | tf_op jit(solution)/shard_map/ppermute | solution.py:14
  332.6 11.4 %collective-permute-start.17 = (f32[3,1,34,1032]{3,2,1,0:T(8,128)S(1)}, f32[3,1,34,1032]{3,2,1,0:T(8,128)S(1)}, u32[]{:S(2)}, u32[]{:S(2)}) collective-permute-start(f32[3,1,34,1032]{3,2,1,0:T(8,128)S(1)} %get-tuple-element.16), channel_id=1, source_target_pairs={{1,0},{3,2},{5,4},{7,6},{9,8},{11,10},{13,12},{15,14},{17,16},{19,... | collective-permute-start | bytes 1263176 | tf_op jit(solution)/shard_map/ppermute | solution.py:17
  347.9 1.7 copy-start.1
  (1 other events, 1.2 us)
Sparse Core Ops, SparseCore 0:
  9.5 75.4 all-gather.2
  86.5 18.3 all-gather.4
  204.4 21.1 all-reduce.7
where the time goes:
time: 357 us; the launch traced here: 356 us
  waiting for transfers between devices  174 us (49%)
  blocking collectives  64.2 us (18%)
  starting transfers between devices  43.5 us (12%)
  local copies, waits for them, and re-layouts  30.2 us (8%)
  other arithmetic  25.1 us (7%)
  between operations  13.6 us (4%)
  matrix products  5.59 us (2%)
    all_gather x1, waiting for transfers between devices, on_device(): column_block = lax.all_gather(own_block, 'row', axis=0, tiled=True)  76.3 us
    all_gather x1, blocking collectives, on_device(): row_whole = lax.all_gather(row_taper, 'row', axis=0, tiled=True)  41.8 us
    ppermute x9, waiting for transfers between devices, extended(): lax.ppermute(lax.slice_in_dim(block, 0, width, axis=dim), axis, backward)  36.1 us
    ppermute x9, starting transfers between devices, extended(): lax.ppermute(lax.slice_in_dim(block, block.shape[dim] - width, None, axis...  25.5 us
    all_to_all x1, blocking collectives, on_device(): lax.all_to_all(tapered.astype(jnp.bfloat16), 'row', split_axis=1, concat_...  22.4 us
    ppermute x9, waiting for transfers between devices, extended(): lax.ppermute(lax.slice_in_dim(block, block.shape[dim] - width, None, axis...  21.8 us
    all_gather x1, waiting for transfers between devices, on_device(): lax.all_gather(column_block, 'mem', axis=1, tiled=True)  19.9 us
    psum x1, waiting for transfers between devices, on_device(): summed = lax.psum(weighted, 'mem')  19.7 us
  transfers between devices with their start and end apart: 22, of which 19 were waited for; matrix products, arithmetic and copies ran while one was open for 2% of the time, Pallas kernels for 0%

commit v1 on v0

v1 whole, which is shorter than its diff:
```python
import jax
import jax.numpy as jnp
from jax import lax
from jax.sharding import PartitionSpec as P

STEPS = 4


def faces(block, axis, dim):
    count = lax.axis_size(axis)
    forward = [(i, i + 1) for i in range(count - 1)]
    backward = [(target, source) for source, target in forward]
    last = block.shape[dim]
    low = lax.ppermute(lax.slice_in_dim(block, last - 1, last, axis=dim), axis, forward)
    high = lax.ppermute(lax.slice_in_dim(block, 0, 1, axis=dim), axis, backward)
    return low, high


def advance(present, courant_numbers, tracer_slope):
    change = 0.0
    ends = [faces(present, axis, dim) for axis, dim in (("lev", 1), ("row", 2), ("mem", 3))]
    for at, (low, high) in enumerate(ends):
        dim = at + 1
        size = present.shape[dim]
        behind = jnp.concatenate([low, lax.slice_in_dim(present, 0, size - 1, axis=dim)], axis=dim)
        forward = jnp.concatenate([lax.slice_in_dim(present, 1, size, axis=dim), high], axis=dim)
        velocity = courant_numbers[at]
        change = change + (
            jnp.maximum(velocity, 0.0) * (present - behind)
            + jnp.minimum(velocity, 0.0) * (forward - present)
        )
    shifted = present - change
    source = present[0] * tracer_slope[0] + present[1] * tracer_slope[1]
    return jnp.concatenate([shifted[:2], shifted[2:] - source[None]], axis=0)


def on_device(
    control_fields, perturbations, column_taper, row_taper, courant_numbers, tracer_slope
):
    member_count, level_count, row_count, column_count = control_fields.shape
    field_count = member_count * level_count
    mem_count = lax.axis_size("mem")
    mem_at = lax.axis_index("mem")
    width = column_count // mem_count
    own_block = lax.dynamic_slice_in_dim(column_taper, mem_at * width, width, 1)
    taper_columns = lax.all_gather(own_block, "row", axis=0, tiled=True)
    row_whole = lax.all_gather(row_taper, "row", axis=0, tiled=True)
    fields = control_fields.reshape(field_count, row_count, column_count)
    tapered = jnp.einsum(
        "ij,fjc->fic",
        row_whole,
        lax.all_to_all(fields, "row", split_axis=2, concat_axis=1, tiled=True),
        preferred_element_type=jnp.float32,
    )
    tapered = lax.all_to_all(
        tapered.astype(jnp.bfloat16), "row", split_axis=1, concat_axis=2, tiled=True
    )
    weighted = 0.0
    for shift in range(mem_count):
        ring = [(i, (i + shift) % mem_count) for i in range(mem_count)]
        target = lax.rem(mem_at + shift, mem_count)
        part = lax.dynamic_slice_in_dim(perturbations, target * width, width, 4)
        half = tapered
        if shift:
            part = lax.ppermute(part, "mem", ring)
            half = lax.ppermute(half, "mem", ring)
        localized = jnp.dot(
            half.reshape(field_count * row_count, column_count),
            taper_columns,
            preferred_element_type=jnp.float32,
        ).reshape(member_count, level_count, row_count, width)
        for m in range(member_count):
            weighted = weighted + part[:, m].astype(jnp.float32) * localized[m][None]
    present = weighted
    for advect_step in range(STEPS):
        present = advance(present, courant_numbers, tracer_slope)
    return present


def solution(mesh):
    placed = (
        P("mem", "lev", "row", None),
        P(None, "mem", "lev", "row", None),
        P("row", None),
        P("row", None),
        P(None, "lev", "row", "mem"),
        P(None, "lev", "row", "mem"),
    )
    return jax.shard_map(
        on_device,
        mesh=mesh,
        in_specs=placed,
        out_specs=P(None, "lev", "row", "mem"),
        check_vma=False,
    )
```

time: 357 us -> 223 us (0.62)
  waiting for transfers between devices: 174 us -> 29.7 us
  starting transfers between devices: 43.5 us -> 71.8 us
  other arithmetic: 25.1 us -> 14.8 us
  blocking collectives: 64.2 us -> 54.5 us
    all_gather x2 -> x1, waiting for transfers between devices: 96.3 us -> 0.01 us  [on_device(): taper_columns = lax.all_gather(own_block, 'row', axis=0, tiled=True)]
    ppermute x18 -> x26, waiting for transfers between devices: 57.9 us -> 3.58 us  [the longest x12 3.55 us: faces(): lax.ppermute(lax.slice_in_dim(block, last - 1, last, axis=dim), axis, for...]
    all_to_all x1 -> x2, waiting for transfers between devices: 0.01 us -> 26.1 us  [the longest x1 26.1 us: on_device(): lax.all_to_all(tapered.astype(jnp.bfloat16), 'row', split_axis=1, concat_...]
    ppermute x18 -> x26, starting transfers between devices: 37.6 us -> 60.8 us  [the longest x12 45.3 us: faces(): lax.ppermute(lax.slice_in_dim(block, last - 1, last, axis=dim), axis, for...]
    all_to_all x1 -> x0, blocking collectives: 22.4 us -> none  [on_device(): lax.all_to_all(tapered.astype(jnp.bfloat16), 'row', split_axis=1, concat_...]
    psum x1 -> x0, waiting for transfers between devices: 19.7 us -> none  [on_device(): summed = lax.psum(weighted, 'mem')]
    all_gather x1, blocking collectives: 41.8 us -> 54.5 us  [on_device(): row_whole = lax.all_gather(row_taper, 'row', axis=0, tiled=True)]
    sub x4, other arithmetic: 12.4 us -> 6.41 us  [advance(): shifted = present - change]
  transfers between devices with their start and end apart: 22 -> 29, of which waited for: 19 -> 6; matrix products, arithmetic and copies ran while one was open for 2% -> 16% of each run, Pallas kernels for 0% -> 0%
where the time goes in v1:
time: 223 us; the launch traced here: 221 us
  starting transfers between devices  71.8 us (32%)
  blocking collectives  54.5 us (24%)
  local copies, waits for them, and re-layouts  30.4 us (14%)
  waiting for transfers between devices  29.7 us (13%)
  other arithmetic  14.8 us (7%)
  between operations  14.1 us (6%)
  matrix products  6.28 us (3%)
    all_gather x1, blocking collectives, on_device(): row_whole = lax.all_gather(row_taper, 'row', axis=0, tiled=True)  54.5 us
    ppermute x12, starting transfers between devices, faces(): lax.ppermute(lax.slice_in_dim(block, last - 1, last, axis=dim), axis, for...  45.3 us
    all_to_all x1, waiting for transfers between devices, on_device(): lax.all_to_all(tapered.astype(jnp.bfloat16), 'row', split_axis=1, concat_...  26.1 us
    ppermute x12, starting transfers between devices, faces(): high = lax.ppermute(lax.slice_in_dim(block, 0, 1, axis=dim), axis, backward)  15.5 us
    unnamed x18, local copies, waits for them, and re-layouts  14.7 us
    all_to_all x1, starting transfers between devices, on_device(): lax.all_to_all(fields, 'row', split_axis=2, concat_axis=1, tiled=True)  7.41 us
    sub x4, other arithmetic, advance(): shifted = present - change  6.41 us
    dot_general x2, matrix products, on_device(): jnp.dot(half.reshape(field_count * row_count, column_count), taper_column...  5.86 us
  transfers between devices with their start and end apart: 29, of which 6 were waited for; matrix products, arithmetic and copies ran while one was open for 16% of the time, Pallas kernels for 0%

profile of v1, /device:TPU:0, one launch (start us, length us, event | category | flops | bytes accessed | tf_op | source)
XLA Modules:
  0.0 221.5 jit_solution(6026272361632896268)
XLA Ops:
  8.6 4.2 %copy.27 = bf16[6,32,2048]{1,0,2:T(8,128)(2,1)} copy(bf16[6,32,2048]{2,1,0:T(8,128)(2,1)S(1)} %bitcast.79) | data formatting | bytes 1572864 | tf_op jit(solution)/shard_map/reshape | solution.py:48
  12.9 5.7 %reshape.36 = bf16[8,2,24576]{2,1,0:T(2,128)(2,1)} reshape(bf16[2048,6,32]{2,1,0:T(8,128)(2,1)} %bitcast.70) | data formatting | bytes 1572864
  18.6 7.4 %all-to-all-start = ((bf16[8,2,24576]{2,1,0:T(2,128)(2,1)}), bf16[8,2,24576]{2,1,0:T(2,128)(2,1)S(1)}, u32[]{:S(2)}, u32[]{:S(2)}) async-start(bf16[8,2,24576]{2,1,0:T(2,128)(2,1)} %reshape.36), calls=%async_computation | async-start | bytes 1572864 | tf_op jit(solution)/shard_map/all_to_all | solution.py:52
  26.0 54.5 %all_gather.6 = bf16[256,256]{1,0:T(8,128)(2,1)S(1)} all-gather(bf16[32,256]{1,0:T(8,128)(2,1)S(1)} %copy-done.6), channel_id=1, replica_groups=mesh['row'=8,'mem'=2,'lev'=2] {'row'}, dimensions={0}, use_global_device_ids=true | all-gather | bytes 147456 | tf_op jit(solution)/shard_map/all_gather | solution.py:47
  80.5 4.2 %reshape.37 = bf16[2048,6,32]{2,1,0:T(8,128)(2,1)} reshape(bf16[8,2,24576]{2,1,0:T(2,128)(2,1)S(1)} %all-to-all-done) | data formatting | bytes 1572864
  84.7 4.2 %copy.29 = bf16[6,8,32,256]{3,2,1,0:T(8,128)(2,1)S(1)} copy(bf16[6,8,32,256]{2,0,3,1:T(8,128)(2,1)} %bitcast.69) | data formatting | bytes 1572864 | tf_op jit(solution)/shard_map/all_to_all | solution.py:52
  89.3 1.8 copy.31
  91.0 3.6 %all-to-all-start.1 = ((bf16[6,256,256]{2,0,1:T(8,128)(2,1)}), bf16[6,256,256]{2,0,1:T(8,128)(2,1)S(1)}, u32[]{:S(2)}, u32[]{:S(2)}) async-start(bf16[6,256,256]{2,0,1:T(8,128)(2,1)} %copy.31), calls=%async_computation.1 | async-start | bytes 2097152 | tf_op jit(solution)/shard_map/all_to_all | solution.py:55
  94.6 1.4 constant_dynamic-slice_fusion
  97.1 26.1 %all-to-all-done.1 = bf16[6,256,256]{2,0,1:T(8,128)(2,1)S(1)} async-done(((bf16[6,256,256]{2,0,1:T(8,128)(2,1)}), bf16[6,256,256]{2,0,1:T(8,128)(2,1)S(1)}, u32[]{:S(2)}, u32[]{:S(2)}) %all-to-all-start.1) | async-done | bytes 786464 | tf_op jit(solution)/shard_map/all_to_all | solution.py:55
  124.9 1.6 maximum_bitcast_fusion.2
  127.7 3.6 %fusion.105 = f32[192,1024]{1,0:T(8,128)S(1)} fusion(bf16[192,2048]{1,0:T(8,128)(2,1)} %bitcast.74, bf16[2048,1024]{1,0:T(8,128)(2,1)} %all-gather.2.cloned.1.call-done), kind=kOutput, calls=%fused_computation.230 | convolution fusion | flops 805306368 | bytes 5767168 | tf_op jit(solution)/shard_map/dot_general | solution.py:67
  131.4 2.3 %fusion.106 = f32[192,1024]{1,0:T(8,128)S(1)} fusion(bf16[192,2048]{1,0:T(8,128)(2,1)} %bitcast.17, bf16[2048,1024]{1,0:T(8,128)(2,1)S(1)} %copy-done.2), kind=kOutput, calls=%fused_computation.231 | convolution fusion | flops 805306368 | bytes 5767168 | tf_op jit(solution)/shard_map/dot_general | solution.py:67
  133.8 1.8 fusion.61
  139.1 4.6 %collective-permute-start.2 = (f32[3,1,32,1024]{3,2,1,0:T(8,128)S(1)}, f32[3,1,32,1024]{3,2,1,0:T(8,128)S(1)}, u32[]{:S(2)}, u32[]{:S(2)}) collective-permute-start(f32[3,1,32,1024]{3,2,1,0:T(8,128)S(1)} %get-tuple-element.58), channel_id=1, source_target_pairs={{0,1},{2,3},{4,5},{6,7},{8,9},{10,11},{12,13},{14,15},{16,17},{18,... | collective-permute-start | bytes 1179656 | tf_op jit(solution)/shard_map/ppermute | solution.py:14
  145.0 4.5 %collective-permute-start.4 = (f32[3,3,1,1024]{3,2,1,0:T(1,128)S(1)}, f32[3,3,1,1024]{3,2,1,0:T(1,128)S(1)}, u32[]{:S(2)}, u32[]{:S(2)}) collective-permute-start(f32[3,3,1,1024]{3,2,1,0:T(1,128)S(1)} %get-tuple-element.54), channel_id=1, source_target_pairs={{0,4},{4,8},{8,12},{12,16},{16,20},{20,24},{24,28},{1,5},{5,9},{9,... | collective-permute-start | bytes 110600 | tf_op jit(solution)/shard_map/ppermute | solution.py:14
  149.6 1.9 collective-permute-start.6
  153.0 1.6 fusion.17
  159.0 4.6 %collective-permute-start.8 = (f32[3,1,32,1024]{3,2,1,0:T(8,128)S(1)}, f32[3,1,32,1024]{3,2,1,0:T(8,128)S(1)}, u32[]{:S(2)}, u32[]{:S(2)}) collective-permute-start(f32[3,1,32,1024]{3,2,1,0:T(8,128)S(1)} %get-tuple-element.40), channel_id=1, source_target_pairs={{0,1},{2,3},{4,5},{6,7},{8,9},{10,11},{12,13},{14,15},{16,17},{18,... | collective-permute-start | bytes 1179656 | tf_op jit(solution)/shard_map/ppermute | solution.py:14
  165.4 4.5 %collective-permute-start.10 = (f32[3,3,1,1024]{3,2,1,0:T(1,128)S(1)}, f32[3,3,1,1024]{3,2,1,0:T(1,128)S(1)}, u32[]{:S(2)}, u32[]{:S(2)}) collective-permute-start(f32[3,3,1,1024]{3,2,1,0:T(1,128)S(1)} %get-tuple-element.36), channel_id=1, source_target_pairs={{0,4},{4,8},{8,12},{12,16},{16,20},{20,24},{24,28},{1,5},{5,9},{9,... | collective-permute-start | bytes 110600 | tf_op jit(solution)/shard_map/ppermute | solution.py:14
  169.9 2.2 %collective-permute-start.12 = (f32[3,3,32,1]{3,2,1,0:T(8,128)S(1)}, f32[3,3,32,1]{3,2,1,0:T(8,128)S(1)}, u32[]{:S(2)}, u32[]{:S(2)}) collective-permute-start(f32[3,3,32,1]{3,2,1,0:T(8,128)S(1)} %get-tuple-element.32), channel_id=1, source_target_pairs={{0,2},{1,3},{4,6},{5,7},{8,10},{9,11},{12,14},{13,15},{16,18},{17,... | collective-permute-start | bytes 3464 | tf_op jit(solution)/shard_map/ppermute | solution.py:14
  173.0 1.6 fusion.29
  175.3 1.3 collective-permute-start.19
  176.6 1.3 collective-permute-start.15
  177.9 4.6 %collective-permute-start.14 = (f32[3,1,32,1024]{3,2,1,0:T(8,128)S(1)}, f32[3,1,32,1024]{3,2,1,0:T(8,128)S(1)}, u32[]{:S(2)}, u32[]{:S(2)}) collective-permute-start(f32[3,1,32,1024]{3,2,1,0:T(8,128)S(1)} %get-tuple-element.28), channel_id=1, source_target_pairs={{0,1},{2,3},{4,5},{6,7},{8,9},{10,11},{12,13},{14,15},{16,17},{18,... | collective-permute-start | bytes 1179656 | tf_op jit(solution)/shard_map/ppermute | solution.py:14
  184.3 4.5 %collective-permute-start.16 = (f32[3,3,1,1024]{3,2,1,0:T(1,128)S(1)}, f32[3,3,1,1024]{3,2,1,0:T(1,128)S(1)}, u32[]{:S(2)}, u32[]{:S(2)}) collective-permute-start(f32[3,3,1,1024]{3,2,1,0:T(1,128)S(1)} %get-tuple-element.24), channel_id=1, source_target_pairs={{0,4},{4,8},{8,12},{12,16},{16,20},{20,24},{24,28},{1,5},{5,9},{9,... | collective-permute-start | bytes 110600 | tf_op jit(solution)/shard_map/ppermute | solution.py:14
  188.9 2.0 collective-permute-start.18
  192.0 1.6 fusion.41
  196.9 4.6 %collective-permute-start.20 = (f32[3,1,32,1024]{3,2,1,0:T(8,128)S(1)}, f32[3,1,32,1024]{3,2,1,0:T(8,128)S(1)}, u32[]{:S(2)}, u32[]{:S(2)}) collective-permute-start(f32[3,1,32,1024]{3,2,1,0:T(8,128)S(1)} %get-tuple-element.16), channel_id=1, source_target_pairs={{0,1},{2,3},{4,5},{6,7},{8,9},{10,11},{12,13},{14,15},{16,17},{18,... | collective-permute-start | bytes 1179656 | tf_op jit(solution)/shard_map/ppermute | solution.py:14
  203.3 4.9 %collective-permute-start.22 = (f32[3,3,1,1024]{3,2,1,0:T(1,128)S(1)}, f32[3,3,1,1024]{3,2,1,0:T(1,128)S(1)}, u32[]{:S(2)}, u32[]{:S(2)}) collective-permute-start(f32[3,3,1,1024]{3,2,1,0:T(1,128)S(1)} %get-tuple-element.12), channel_id=1, source_target_pairs={{0,4},{4,8},{8,12},{12,16},{16,20},{20,24},{24,28},{1,5},{5,9},{9,... | collective-permute-start | bytes 110600 | tf_op jit(solution)/shard_map/ppermute | solution.py:14
  208.2 2.2 collective-permute-start.24
  211.4 1.6 fusion.53
  (97 shorter events, 30.9 us)
Async XLA Ops:
  6.5 121.2 %all-gather.2.cloned.1.call-start = ((), (), s32[]{:S(2)}) async-start(), calls=%async_computation.2 | async-start | bytes 4718592 | tf_op jit(solution)/shard_map/all_gather | solution.py:46
  18.6 7.4 %copy-start.6 = (bf16[32,256]{1,0:T(8,128)(2,1)S(1)}, bf16[32,256]{1,0:T(8,128)(2,1)}, u32[]{:S(2)}) copy-start(bf16[32,256]{1,0:T(8,128)(2,1)} %param.9) | copy-start | bytes 49156
  18.6 61.9 %all-to-all-start = ((bf16[8,2,24576]{2,1,0:T(2,128)(2,1)}), bf16[8,2,24576]{2,1,0:T(2,128)(2,1)S(1)}, u32[]{:S(2)}, u32[]{:S(2)}) async-start(bf16[8,2,24576]{2,1,0:T(2,128)(2,1)} %reshape.36), calls=%async_computation | async-start | bytes 1572864 | tf_op jit(solution)/shard_map/all_to_all | solution.py:52
  91.0 32.2 %all-to-all-start.1 = ((bf16[6,256,256]{2,0,1:T(8,128)(2,1)}), bf16[6,256,256]{2,0,1:T(8,128)(2,1)S(1)}, u32[]{:S(2)}, u32[]{:S(2)}) async-start(bf16[6,256,256]{2,0,1:T(8,128)(2,1)} %copy.31), calls=%async_computation.1 | async-start | bytes 2097152 | tf_op jit(solution)/shard_map/all_to_all | solution.py:55
  97.1 36.6 %collective-permute-start = (bf16[3,2,3,32,1024]{4,3,2,0,1:T(8,128)(2,1)}, bf16[3,2,3,32,1024]{4,3,2,0,1:T(8,128)(2,1)}, u32[]{:S(2)}, u32[]{:S(2)}) collective-permute-start(bf16[3,2,3,32,1024]{4,3,2,0,1:T(8,128)(2,1)} %copy.44), channel_id=1, source_target_pairs={{0,2},{2,0},{1,3},{3,1},{4,6},{6,4},{5,7},{7,5},{8,10},{10,8},{9,1... | collective-permute-start | bytes 3538952 | tf_op jit(solution)/shard_map/ppermute | solution.py:65
  124.9 6.4 %collective-permute-start.1 = (bf16[6,32,2048]{2,1,0:T(8,128)(2,1)}, bf16[6,32,2048]{2,1,0:T(8,128)(2,1)}, u32[]{:S(2)}, u32[]{:S(2)}) collective-permute-start(bf16[6,32,2048]{2,1,0:T(8,128)(2,1)} %all_to_all.33), channel_id=1, source_target_pairs={{0,2},{2,0},{1,3},{3,1},{4,6},{6,4},{5,7},{7,5},{8,10},{10,8},{9,1... | collective-permute-start | bytes 2359304 | tf_op jit(solution)/shard_map/ppermute | solution.py:66
  127.7 3.7 %copy-start.2 = (bf16[2048,1024]{1,0:T(8,128)(2,1)S(1)}, bf16[2048,1024]{1,0:T(8,128)(2,1)}, u32[]{:S(2)}) copy-start(bf16[2048,1024]{1,0:T(8,128)(2,1)} %all-gather.2.cloned.1.call-done) | copy-start | bytes 12582916
  131.4 2.4 %copy-start.4 = (bf16[3,2,3,32,2048]{4,3,2,1,0:T(8,128)(2,1)S(1)}, bf16[3,2,3,32,2048]{4,3,2,1,0:T(8,128)(2,1)}, u32[]{:S(2)}) copy-start(bf16[3,2,3,32,2048]{4,3,2,1,0:T(8,128)(2,1)} %param.7) | copy-start | bytes 7077892
  136.5 13.1 %collective-permute-start.7 = (f32[3,3,32,1]{3,2,1,0:T(8,128)S(1)}, f32[3,3,32,1]{3,2,1,0:T(8,128)S(1)}, u32[]{:S(2)}, u32[]{:S(2)}) collective-permute-start(f32[3,3,32,1]{3,2,1,0:T(8,128)S(1)} %get-tuple-element.49), channel_id=1, source_target_pairs={{2,0},{3,1},{6,4},{7,5},{10,8},{11,9},{14,12},{15,13},{18,16},{19,... | collective-permute-start | bytes 3464 | tf_op jit(solution)/shard_map/ppermute | solution.py:15
  137.8 14.8 %collective-permute-start.3 = (f32[3,1,32,1024]{3,2,1,0:T(8,128)S(1)}, f32[3,1,32,1024]{3,2,1,0:T(8,128)S(1)}, u32[]{:S(2)}, u32[]{:S(2)}) collective-permute-start(f32[3,1,32,1024]{3,2,1,0:T(8,128)S(1)} %get-tuple-element.57), channel_id=1, source_target_pairs={{1,0},{3,2},{5,4},{7,6},{9,8},{11,10},{13,12},{15,14},{17,16},{19,... | collective-permute-start | bytes 1179656 | tf_op jit(solution)/shard_map/ppermute | solution.py:15
  139.1 13.9 %collective-permute-start.2 = (f32[3,1,32,1024]{3,2,1,0:T(8,128)S(1)}, f32[3,1,32,1024]{3,2,1,0:T(8,128)S(1)}, u32[]{:S(2)}, u32[]{:S(2)}) collective-permute-start(f32[3,1,32,1024]{3,2,1,0:T(8,128)S(1)} %get-tuple-element.58), channel_id=1, source_target_pairs={{0,1},{2,3},{4,5},{6,7},{8,9},{10,11},{12,13},{14,15},{16,17},{18,... | collective-permute-start | bytes 1179656 | tf_op jit(solution)/shard_map/ppermute | solution.py:14
  143.7 8.8 %collective-permute-start.5 = (f32[3,3,1,1024]{3,2,1,0:T(1,128)S(1)}, f32[3,3,1,1024]{3,2,1,0:T(1,128)S(1)}, u32[]{:S(2)}, u32[]{:S(2)}) collective-permute-start(f32[3,3,1,1024]{3,2,1,0:T(1,128)S(1)} %get-tuple-element.53), channel_id=1, source_target_pairs={{4,0},{8,4},{12,8},{16,12},{20,16},{24,20},{28,24},{5,1},{9,5},{13... | collective-permute-start | bytes 110600 | tf_op jit(solution)/shard_map/ppermute | solution.py:15
  145.0 7.5 %collective-permute-start.4 = (f32[3,3,1,1024]{3,2,1,0:T(1,128)S(1)}, f32[3,3,1,1024]{3,2,1,0:T(1,128)S(1)}, u32[]{:S(2)}, u32[]{:S(2)}) collective-permute-start(f32[3,3,1,1024]{3,2,1,0:T(1,128)S(1)} %get-tuple-element.54), channel_id=1, source_target_pairs={{0,4},{4,8},{8,12},{12,16},{16,20},{20,24},{24,28},{1,5},{5,9},{9,... | collective-permute-start | bytes 110600 | tf_op jit(solution)/shard_map/ppermute | solution.py:14
  149.6 2.9 %collective-permute-start.6 = (f32[3,3,32,1]{3,2,1,0:T(8,128)S(1)}, f32[3,3,32,1]{3,2,1,0:T(8,128)S(1)}, u32[]{:S(2)}, u32[]{:S(2)}) collective-permute-start(f32[3,3,32,1]{3,2,1,0:T(8,128)S(1)} %get-tuple-element.50), channel_id=1, source_target_pairs={{0,2},{1,3},{4,6},{5,7},{8,10},{9,11},{12,14},{13,15},{16,18},{17,... | collective-permute-start | bytes 3464 | tf_op jit(solution)/shard_map/ppermute | solution.py:14
  156.4 13.6 %collective-permute-start.13 = (f32[3,3,32,1]{3,2,1,0:T(8,128)S(1)}, f32[3,3,32,1]{3,2,1,0:T(8,128)S(1)}, u32[]{:S(2)}, u32[]{:S(2)}) collective-permute-start(f32[3,3,32,1]{3,2,1,0:T(8,128)S(1)} %get-tuple-element.31), channel_id=1, source_target_pairs={{2,0},{3,1},{6,4},{7,5},{10,8},{11,9},{14,12},{15,13},{18,16},{19,... | collective-permute-start | bytes 3464 | tf_op jit(solution)/shard_map/ppermute | solution.py:15
  157.7 15.3 %collective-permute-start.9 = (f32[3,1,32,1024]{3,2,1,0:T(8,128)S(1)}, f32[3,1,32,1024]{3,2,1,0:T(8,128)S(1)}, u32[]{:S(2)}, u32[]{:S(2)}) collective-permute-start(f32[3,1,32,1024]{3,2,1,0:T(8,128)S(1)} %get-tuple-element.39), channel_id=1, source_target_pairs={{1,0},{3,2},{5,4},{7,6},{9,8},{11,10},{13,12},{15,14},{17,16},{19,... | collective-permute-start | bytes 1179656 | tf_op jit(solution)/shard_map/ppermute | solution.py:15
  159.0 14.1 %collective-permute-start.8 = (f32[3,1,32,1024]{3,2,1,0:T(8,128)S(1)}, f32[3,1,32,1024]{3,2,1,0:T(8,128)S(1)}, u32[]{:S(2)}, u32[]{:S(2)}) collective-permute-start(f32[3,1,32,1024]{3,2,1,0:T(8,128)S(1)} %get-tuple-element.40), channel_id=1, source_target_pairs={{0,1},{2,3},{4,5},{6,7},{8,9},{10,11},{12,13},{14,15},{16,17},{18,... | collective-permute-start | bytes 1179656 | tf_op jit(solution)/shard_map/ppermute | solution.py:14
  164.1 8.9 %collective-permute-start.11 = (f32[3,3,1,1024]{3,2,1,0:T(1,128)S(1)}, f32[3,3,1,1024]{3,2,1,0:T(1,128)S(1)}, u32[]{:S(2)}, u32[]{:S(2)}) collective-permute-start(f32[3,3,1,1024]{3,2,1,0:T(1,128)S(1)} %get-tuple-element.35), channel_id=1, source_target_pairs={{4,0},{8,4},{12,8},{16,12},{20,16},{24,20},{28,24},{5,1},{9,5},{13... | collective-permute-start | bytes 110600 | tf_op jit(solution)/shard_map/ppermute | solution.py:15
  165.4 7.6 %collective-permute-start.10 = (f32[3,3,1,1024]{3,2,1,0:T(1,128)S(1)}, f32[3,3,1,1024]{3,2,1,0:T(1,128)S(1)}, u32[]{:S(2)}, u32[]{:S(2)}) collective-permute-start(f32[3,3,1,1024]{3,2,1,0:T(1,128)S(1)} %get-tuple-element.36), channel_id=1, source_target_pairs={{0,4},{4,8},{8,12},{12,16},{16,20},{20,24},{24,28},{1,5},{5,9},{9,... | collective-permute-start | bytes 110600 | tf_op jit(solution)/shard_map/ppermute | solution.py:14
  169.9 3.0 %collective-permute-start.12 = (f32[3,3,32,1]{3,2,1,0:T(8,128)S(1)}, f32[3,3,32,1]{3,2,1,0:T(8,128)S(1)}, u32[]{:S(2)}, u32[]{:S(2)}) collective-permute-start(f32[3,3,32,1]{3,2,1,0:T(8,128)S(1)} %get-tuple-element.32), channel_id=1, source_target_pairs={{0,2},{1,3},{4,6},{5,7},{8,10},{9,11},{12,14},{13,15},{16,18},{17,... | collective-permute-start | bytes 3464 | tf_op jit(solution)/shard_map/ppermute | solution.py:14
  175.3 13.6 %collective-permute-start.19 = (f32[3,3,32,1]{3,2,1,0:T(8,128)S(1)}, f32[3,3,32,1]{3,2,1,0:T(8,128)S(1)}, u32[]{:S(2)}, u32[]{:S(2)}) collective-permute-start(f32[3,3,32,1]{3,2,1,0:T(8,128)S(1)} %get-tuple-element.19), channel_id=1, source_target_pairs={{2,0},{3,1},{6,4},{7,5},{10,8},{11,9},{14,12},{15,13},{18,16},{19,... | collective-permute-start | bytes 3464 | tf_op jit(solution)/shard_map/ppermute | solution.py:15
  176.6 15.3 %collective-permute-start.15 = (f32[3,1,32,1024]{3,2,1,0:T(8,128)S(1)}, f32[3,1,32,1024]{3,2,1,0:T(8,128)S(1)}, u32[]{:S(2)}, u32[]{:S(2)}) collective-permute-start(f32[3,1,32,1024]{3,2,1,0:T(8,128)S(1)} %get-tuple-element.27), channel_id=1, source_target_pairs={{1,0},{3,2},{5,4},{7,6},{9,8},{11,10},{13,12},{15,14},{17,16},{19,... | collective-permute-start | bytes 1179656 | tf_op jit(solution)/shard_map/ppermute | solution.py:15
  177.9 14.1 %collective-permute-start.14 = (f32[3,1,32,1024]{3,2,1,0:T(8,128)S(1)}, f32[3,1,32,1024]{3,2,1,0:T(8,128)S(1)}, u32[]{:S(2)}, u32[]{:S(2)}) collective-permute-start(f32[3,1,32,1024]{3,2,1,0:T(8,128)S(1)} %get-tuple-element.28), channel_id=1, source_target_pairs={{0,1},{2,3},{4,5},{6,7},{8,9},{10,11},{12,13},{14,15},{16,17},{18,... | collective-permute-start | bytes 1179656 | tf_op jit(solution)/shard_map/ppermute | solution.py:14
  183.0 8.9 %collective-permute-start.17 = (f32[3,3,1,1024]{3,2,1,0:T(1,128)S(1)}, f32[3,3,1,1024]{3,2,1,0:T(1,128)S(1)}, u32[]{:S(2)}, u32[]{:S(2)}) collective-permute-start(f32[3,3,1,1024]{3,2,1,0:T(1,128)S(1)} %get-tuple-element.23), channel_id=1, source_target_pairs={{4,0},{8,4},{12,8},{16,12},{20,16},{24,20},{28,24},{5,1},{9,5},{13... | collective-permute-start | bytes 110600 | tf_op jit(solution)/shard_map/ppermute | solution.py:15
  184.3 7.6 %collective-permute-start.16 = (f32[3,3,1,1024]{3,2,1,0:T(1,128)S(1)}, f32[3,3,1,1024]{3,2,1,0:T(1,128)S(1)}, u32[]{:S(2)}, u32[]{:S(2)}) collective-permute-start(f32[3,3,1,1024]{3,2,1,0:T(1,128)S(1)} %get-tuple-element.24), channel_id=1, source_target_pairs={{0,4},{4,8},{8,12},{12,16},{16,20},{20,24},{24,28},{1,5},{5,9},{9,... | collective-permute-start | bytes 110600 | tf_op jit(solution)/shard_map/ppermute | solution.py:14
  188.9 3.0 %collective-permute-start.18 = (f32[3,3,32,1]{3,2,1,0:T(8,128)S(1)}, f32[3,3,32,1]{3,2,1,0:T(8,128)S(1)}, u32[]{:S(2)}, u32[]{:S(2)}) collective-permute-start(f32[3,3,32,1]{3,2,1,0:T(8,128)S(1)} %get-tuple-element.20), channel_id=1, source_target_pairs={{0,2},{1,3},{4,6},{5,7},{8,10},{9,11},{12,14},{13,15},{16,18},{17,... | collective-permute-start | bytes 3464 | tf_op jit(solution)/shard_map/ppermute | solution.py:14
  194.3 13.9 %collective-permute-start.25 = (f32[3,3,32,1]{3,2,1,0:T(8,128)S(1)}, f32[3,3,32,1]{3,2,1,0:T(8,128)S(1)}, u32[]{:S(2)}, u32[]{:S(2)}) collective-permute-start(f32[3,3,32,1]{3,2,1,0:T(8,128)S(1)} %get-tuple-element.7), channel_id=1, source_target_pairs={{2,0},{3,1},{6,4},{7,5},{10,8},{11,9},{14,12},{15,13},{18,16},{19,... | collective-permute-start | bytes 3464 | tf_op jit(solution)/shard_map/ppermute | solution.py:15
  195.6 15.8 %collective-permute-start.21 = (f32[3,1,32,1024]{3,2,1,0:T(8,128)S(1)}, f32[3,1,32,1024]{3,2,1,0:T(8,128)S(1)}, u32[]{:S(2)}, u32[]{:S(2)}) collective-permute-start(f32[3,1,32,1024]{3,2,1,0:T(8,128)S(1)} %get-tuple-element.15), channel_id=1, source_target_pairs={{1,0},{3,2},{5,4},{7,6},{9,8},{11,10},{13,12},{15,14},{17,16},{19,... | collective-permute-start | bytes 1179656 | tf_op jit(solution)/shard_map/ppermute | solution.py:15
  196.9 14.5 %collective-permute-start.20 = (f32[3,1,32,1024]{3,2,1,0:T(8,128)S(1)}, f32[3,1,32,1024]{3,2,1,0:T(8,128)S(1)}, u32[]{:S(2)}, u32[]{:S(2)}) collective-permute-start(f32[3,1,32,1024]{3,2,1,0:T(8,128)S(1)} %get-tuple-element.16), channel_id=1, source_target_pairs={{0,1},{2,3},{4,5},{6,7},{8,9},{10,11},{12,13},{14,15},{16,17},{18,... | collective-permute-start | bytes 1179656 | tf_op jit(solution)/shard_map/ppermute | solution.py:14
  202.0 9.4 %collective-permute-start.23 = (f32[3,3,1,1024]{3,2,1,0:T(1,128)S(1)}, f32[3,3,1,1024]{3,2,1,0:T(1,128)S(1)}, u32[]{:S(2)}, u32[]{:S(2)}) collective-permute-start(f32[3,3,1,1024]{3,2,1,0:T(1,128)S(1)} %get-tuple-element.11), channel_id=1, source_target_pairs={{4,0},{8,4},{12,8},{16,12},{20,16},{24,20},{28,24},{5,1},{9,5},{13... | collective-permute-start | bytes 110600 | tf_op jit(solution)/shard_map/ppermute | solution.py:15
  203.3 8.1 %collective-permute-start.22 = (f32[3,3,1,1024]{3,2,1,0:T(1,128)S(1)}, f32[3,3,1,1024]{3,2,1,0:T(1,128)S(1)}, u32[]{:S(2)}, u32[]{:S(2)}) collective-permute-start(f32[3,3,1,1024]{3,2,1,0:T(1,128)S(1)} %get-tuple-element.12), channel_id=1, source_target_pairs={{0,4},{4,8},{8,12},{12,16},{16,20},{20,24},{24,28},{1,5},{5,9},{9,... | collective-permute-start | bytes 110600 | tf_op jit(solution)/shard_map/ppermute | solution.py:14
  208.2 3.2 %collective-permute-start.24 = (f32[3,3,32,1]{3,2,1,0:T(8,128)S(1)}, f32[3,3,32,1]{3,2,1,0:T(8,128)S(1)}, u32[]{:S(2)}, u32[]{:S(2)}) collective-permute-start(f32[3,3,32,1]{3,2,1,0:T(8,128)S(1)} %get-tuple-element.8), channel_id=1, source_target_pairs={{0,2},{1,3},{4,6},{5,7},{8,10},{9,11},{12,14},{13,15},{16,18},{17,... | collective-permute-start | bytes 3464 | tf_op jit(solution)/shard_map/ppermute | solution.py:14
  (4 other events, 5.9 us)
Sparse Core Ops, SparseCore 0:
  9.5 96.5 all-gather.1

commit v2 on v1

--- a/solution.py
+++ b/solution.py
@@ -1,37 +1,212 @@
 import jax
 import jax.numpy as jnp
 from jax import lax
+from jax.experimental import pallas as pl
+from jax.experimental.pallas import tpu as pltpu
 from jax.sharding import PartitionSpec as P
 
 STEPS = 4
 
 
-def faces(block, axis, dim):
-    count = lax.axis_size(axis)
-    forward = [(i, i + 1) for i in range(count - 1)]
-    backward = [(target, source) for source, target in forward]
-    last = block.shape[dim]
-    low = lax.ppermute(lax.slice_in_dim(block, last - 1, last, axis=dim), axis, forward)
-    high = lax.ppermute(lax.slice_in_dim(block, 0, 1, axis=dim), axis, backward)
-    return low, high
-
-
-def advance(present, courant_numbers, tracer_slope):
-    change = 0.0
-    ends = [faces(present, axis, dim) for axis, dim in (("lev", 1), ("row", 2), ("mem", 3))]
-    for at, (low, high) in enumerate(ends):
-        dim = at + 1
-        size = present.shape[dim]
-        behind = jnp.concatenate([low, lax.slice_in_dim(present, 0, size - 1, axis=dim)], axis=dim)
-        forward = jnp.concatenate([lax.slice_in_dim(present, 1, size, axis=dim), high], axis=dim)
-        velocity = courant_numbers[at]
-        change = change + (
-            jnp.maximum(velocity, 0.0) * (present - behind)
-            + jnp.minimum(velocity, 0.0) * (forward - present)
+MESH = pl.DeviceIdType.MESH
+AXES = ("lev", "row", "mem")
+
+
+def sides():
+    found = []
+    for at, axis in enumerate(AXES):
+        here, count = lax.axis_index(axis), lax.axis_size(axis)
+        if count > 1:
+            found.append((at, 0, axis, here > 0, here - 1))
+            found.append((at, 1, axis, here < count - 1, here + 1))
+    return found
+
+
+def advect_kernel(
+    first, courant, slope, out, state, factors, level_send, row_send, level_halo, row_halo,
+    column_halo, send_sem, recv_sem,
+):
+    kinds, levels, rows, width = first.shape
+    barrier = pltpu.get_barrier_semaphore()
+    neighbours = sides()
+    for at, side, axis, there, target in neighbours:
+
+        @pl.when(there)
+        def _():
+            pl.semaphore_signal(barrier, inc=1, device_id={axis: target}, device_id_type=MESH)
+
+    row_at = lax.broadcasted_iota(jnp.int32, (rows, width), 0)
+    column_at = lax.broadcasted_iota(jnp.int32, (rows, width), 1)
+    for level in range(levels):
+        centre = jnp.ones((rows, width), jnp.float32)
+        for at in range(3):
+            ahead = jnp.maximum(courant[at, level], 0.0)
+            back = jnp.minimum(courant[at, level], 0.0)
+            centre = centre - ahead + back
+            if at == 1:
+                ahead = jnp.where(row_at == 0, 0.0, ahead)
+                back = jnp.where(row_at == rows - 1, 0.0, back)
+            if at == 2:
+                ahead = jnp.where(column_at == 0, 0.0, ahead)
+                back = jnp.where(column_at == width - 1, 0.0, back)
+            factors[1 + 2 * at, level] = ahead
+            factors[2 + 2 * at, level] = back
+        factors[0, level] = centre
+    for kind in range(kinds):
+        for level in range(levels):
+            state[0, kind, level] = first[kind, level]
+    pl.semaphore_wait(barrier, sum(there.astype(jnp.int32) for _, _, _, there, _ in neighbours))
+
+    def copy_of(step, at, side, axis, target):
+        if at == 0:
+            source, landing = level_send.at[step, side], level_halo.at[step, 1 - side]
+        elif at == 1:
+            source, landing = row_send.at[step, side], row_halo.at[step, 1 - side]
+        else:
+            lanes = pl.ds(0 if side == 0 else width - 128, 128)
+            source = state.at[step, :, :, :, lanes]
+            landing = column_halo.at[step, 1 - side]
+        return pltpu.make_async_remote_copy(
+            src_ref=source,
+            dst_ref=landing,
+            send_sem=send_sem.at[step, 2 * at + side],
+            recv_sem=recv_sem.at[step, 2 * at + 1 - side],
+            device_id={axis: target},
+            device_id_type=MESH,
         )
-    shifted = present - change
-    source = present[0] * tracer_slope[0] + present[1] * tracer_slope[1]
-    return jnp.concatenate([shifted[:2], shifted[2:] - source[None]], axis=0)
+
+    def arrival(step, at, side, axis, target):
+        landing = (level_halo, row_halo, column_halo)[at].at[step, side]
+        return pltpu.make_async_remote_copy(
+            src_ref=landing,
+            dst_ref=landing,
+            send_sem=send_sem.at[step, 2 * at + side],
+            recv_sem=recv_sem.at[step, 2 * at + side],
+            device_id={axis: target},
+            device_id_type=MESH,
+        )
+
+    def one_step(step, target_ref):
+        for at, side, axis, there, target in neighbours:
+
+            @pl.when(there)
+            def _():
+                for kind in range(kinds):
+                    if at == 0:
+                        level_send[step, side, kind] = state[
+                            step, kind, 0 if side == 0 else levels - 1
+                        ].astype(level_send.dtype)
+                    if at == 1:
+                        edge = 0 if side == 0 else rows - 1
+                        for level in range(levels):
+                            row_send[step, side, pl.ds(kind * levels + level, 1)] = state[
+                                step, kind, level, pl.ds(edge, 1)
+                            ]
+                copy_of(step, at, side, axis, target).start()
+
+        for level in range(levels):
+            for kind in range(kinds):
+                here = state[step, kind, level]
+                new = here * factors[0, level]
+                new = new + factors[3, level] * pltpu.roll(here, 1, 0)
+                new = new - factors[4, level] * pltpu.roll(here, rows - 1, 0)
+                new = new + factors[5, level] * pltpu.roll(here, 1, 1)
+                new = new - factors[6, level] * pltpu.roll(here, width - 1, 1)
+                if level > 0:
+                    new = new + factors[1, level] * state[step, kind, level - 1]
+                if level < levels - 1:
+                    new = new - factors[2, level] * state[step, kind, level + 1]
+                if kind == 2:
+                    new = new - (
+                        state[step, 0, level] * slope[0, level]
+                        + state[step, 1, level] * slope[1, level]
+                    )
+                target_ref[kind, level] = new
+
+        lane_at = lax.broadcasted_iota(jnp.int32, (rows, 128), 1)
+        for at, side, axis, there, target in (
+            [n for n in neighbours if n[0] == 2]
+            + [n for n in neighbours if n[0] == 1]
+            + [n for n in neighbours if n[0] == 0]
+        ):
+
+            @pl.when(there)
+            def _():
+                arrival(step, at, side, axis, target).wait_recv()
+                for kind in range(kinds):
+                    if at == 0:
+                        level = 0 if side == 0 else levels - 1
+                        term = factors[1 + side, level] * level_halo[step, side, kind].astype(
+                            jnp.float32
+                        )
+                        if side:
+                            term = -term
+                        target_ref[kind, level] = target_ref[kind, level] + term
+                        continue
+                    for level in range(levels):
+                        if at == 1:
+                            edge = pl.ds(0 if side == 0 else rows - 1, 1)
+                            speed = courant[1, level, edge]
+                            speed = jnp.minimum(speed, 0.0) if side else jnp.maximum(speed, 0.0)
+                            term = speed * row_halo[step, side, pl.ds(kind * levels + level, 1)]
+                            if side:
+                                term = -term
+                            target_ref[kind, level, edge] = target_ref[kind, level, edge] + term
+                        else:
+                            lanes = pl.ds(width - 128 if side else 0, 128)
+                            speed = courant[2, level, :, lanes]
+                            speed = jnp.minimum(speed, 0.0) if side else jnp.maximum(speed, 0.0)
+                            beside = pltpu.roll(
+                                column_halo[step, side, kind, level], 127 if side else 1, 1
+                            )
+                            term = jnp.where(
+                                lane_at == (127 if side else 0), speed * beside, 0.0
+                            )
+                            if side:
+                                term = -term
+                            target_ref[kind, level, :, lanes] = (
+                                target_ref[kind, level, :, lanes] + term
+                            )
+
+    @pl.loop(0, STEPS - 1)
+    def _(step):
+        one_step(step, state.at[step + 1])
+
+    one_step(STEPS - 1, out)
+
+    @pl.loop(0, STEPS)
+    def _(step):
+        for at, side, axis, there, target in neighbours:
+
+            @pl.when(there)
+            def _():
+                copy_of(step, at, side, axis, target).wait_send()
+
+
+def advected(weighted, courant_numbers, tracer_slope):
+    kinds, levels, rows, width = weighted.shape
+    edges = -(-kinds * levels // 8) * 8
+    return pl.pallas_call(
+        advect_kernel,
+        out_shape=jax.ShapeDtypeStruct(weighted.shape, jnp.float32),
+        in_specs=[pl.BlockSpec(memory_space=pltpu.VMEM)] * 3,
+        out_specs=pl.BlockSpec(memory_space=pltpu.VMEM),
+        scratch_shapes=[
+            pltpu.VMEM((STEPS, kinds, levels, rows, width), jnp.float32),
+            pltpu.VMEM((7, levels, rows, width), jnp.float32),
+            pltpu.VMEM((STEPS, 2, kinds, rows, width), jnp.bfloat16),
+            pltpu.VMEM((STEPS, 2, edges, width), jnp.float32),
+            pltpu.VMEM((STEPS, 2, kinds, rows, width), jnp.bfloat16),
+            pltpu.VMEM((STEPS, 2, edges, width), jnp.float32),
+            pltpu.VMEM((STEPS, 2, kinds, levels, rows, 128), jnp.float32),
+            pltpu.SemaphoreType.DMA((STEPS, 6)),
+            pltpu.SemaphoreType.DMA((STEPS, 6)),
+        ],
+        compiler_params=pltpu.CompilerParams(
+            collective_id=1, has_side_effects=True, vmem_limit_bytes=48 << 20
+        ),
+        name="advect",
+    )(weighted, courant_numbers, tracer_slope)
 
 
 def on_device(
@@ -71,10 +246,7 @@
         ).reshape(member_count, level_count, row_count, width)
         for m in range(member_count):
             weighted = weighted + part[:, m].astype(jnp.float32) * localized[m][None]
-    present = weighted
-    for advect_step in range(STEPS):
-        present = advance(present, courant_numbers, tracer_slope)
-    return present
+    return advected(weighted, courant_numbers, tracer_slope)
 
 
 def solution(mesh):

time: 223 us -> 166 us (0.74)
  starting transfers between devices: 71.8 us -> 7.97 us
  blocking collectives: 54.5 us -> 87.5 us
  waiting for transfers between devices: 29.7 us -> 0.05 us
  Pallas kernels: 0 us -> 22.7 us
  other arithmetic: 14.8 us -> 1.92 us
  local copies, waits for them, and re-layouts: 30.4 us -> 26.5 us
    ppermute x24 -> x0, starting transfers between devices: 60.8 us -> none  [the longest x12 45.3 us: faces(): lax.ppermute(lax.slice_in_dim(block, last - 1, last, axis=dim), axis, for...]
    all_to_all x0 -> x1, blocking collectives: none -> 33 us  [on_device(): lax.all_to_all(tapered.astype(jnp.bfloat16), 'row', split_axis=1, concat_...]
    all_to_all x1 -> x0, waiting for transfers between devices: 26.1 us -> none  [on_device(): lax.all_to_all(tapered.astype(jnp.bfloat16), 'row', split_axis=1, concat_...]
    pallas_call x0 -> x1, Pallas kernels: none -> 22.7 us  [advected(): pl.pallas_call(advect_kernel, out_shape=jax.ShapeDtypeStruct(weighted.sha...]
    sub x8 -> x0, other arithmetic: 6.95 us -> none  [the longest x4 6.41 us: advance(): shifted = present - change]
    concatenate x19 -> x0, other arithmetic: 4.51 us -> none  [advance(): return jnp.concatenate([shifted[:2], shifted[2:] - source[None]], axis=0)]
    ppermute x24 -> x0, waiting for transfers between devices: 3.58 us -> none  [the longest x12 3.55 us: faces(): lax.ppermute(lax.slice_in_dim(block, last - 1, last, axis=dim), axis, for...]
    all_to_all x1 -> x0, starting transfers between devices: 3.56 us -> none  [on_device(): lax.all_to_all(tapered.astype(jnp.bfloat16), 'row', split_axis=1, concat_...]
  transfers between devices with their start and end apart: 29 -> 4, of which waited for: 6 -> 0; matrix products, arithmetic and copies ran while one was open for 16% -> 17% of each run, Pallas kernels for 0% -> 0%
where the time goes in v2:
time: 166 us; the launch traced here: 165 us
  blocking collectives  87.5 us (53%)
  local copies, waits for them, and re-layouts  26.5 us (16%)
  Pallas kernels  22.7 us (14%)
  between operations  13.6 us (8%)
  starting transfers between devices  7.97 us (5%)
  matrix products  4.99 us (3%)
  other arithmetic  1.92 us (1%)
    all_gather x1, blocking collectives, on_device(): row_whole = lax.all_gather(row_taper, 'row', axis=0, tiled=True)  54.5 us
    all_to_all x1, blocking collectives, on_device(): lax.all_to_all(tapered.astype(jnp.bfloat16), 'row', split_axis=1, concat_...  33 us
    pallas_call x1, Pallas kernels, advected(): pl.pallas_call(advect_kernel, out_shape=jax.ShapeDtypeStruct(weighted.sha...  22.7 us
    unnamed x19, local copies, waits for them, and re-layouts  14 us
    all_to_all x1, starting transfers between devices, on_device(): lax.all_to_all(fields, 'row', split_axis=2, concat_axis=1, tiled=True)  7.41 us
    dot_general x2, matrix products, on_device(): jnp.dot(half.reshape(field_count * row_count, column_count), taper_column...  4.58 us
    reshape x1, local copies, waits for them, and re-layouts, on_device(): fields = control_fields.reshape(field_count, row_count, column_count)  4.21 us
    all_to_all x1, local copies, waits for them, and re-layouts, on_device(): lax.all_to_all(fields, 'row', split_axis=2, concat_axis=1, tiled=True)  4.17 us
  transfers between devices with their start and end apart: 4, of which 0 were waited for; matrix products, arithmetic and copies ran while one was open for 17% of the time, Pallas kernels for 0%

profile of v2, /device:TPU:0, one launch (start us, length us, event | category | flops | bytes accessed | tf_op | source)
XLA Modules:
  0.0 165.2 jit_solution(225550002045984125)
XLA Ops:
  6.5 1.2 copy-done
  7.8 0.9 constant_dynamic-slice_fusion.1
  8.6 0.0 all-gather.2.cloned.1.call-update
  8.7 4.2 %copy.27 = bf16[6,32,2048]{1,0,2:T(8,128)(2,1)} copy(bf16[6,32,2048]{2,1,0:T(8,128)(2,1)S(1)} %bitcast.67) | data formatting | bytes 1572864 | tf_op jit(solution)/shard_map/reshape | solution.py:223
  12.9 5.7 %reshape.36 = bf16[8,2,24576]{2,1,0:T(2,128)(2,1)} reshape(bf16[2048,6,32]{2,1,0:T(8,128)(2,1)} %bitcast.58) | data formatting | bytes 1572864
  18.6 7.4 %all-to-all-start = ((bf16[8,2,24576]{2,1,0:T(2,128)(2,1)}), bf16[8,2,24576]{2,1,0:T(2,128)(2,1)S(1)}, u32[]{:S(2)}, u32[]{:S(2)}) async-start(bf16[8,2,24576]{2,1,0:T(2,128)(2,1)} %reshape.36), calls=%async_computation | async-start | bytes 1572864 | tf_op jit(solution)/shard_map/all_to_all | solution.py:227
  26.0 54.5 %all_gather.6 = bf16[256,256]{1,0:T(8,128)(2,1)S(1)} all-gather(bf16[32,256]{1,0:T(8,128)(2,1)S(1)} %copy-done.6), channel_id=1, replica_groups=mesh['row'=8,'mem'=2,'lev'=2] {'row'}, dimensions={0}, use_global_device_ids=true | all-gather | bytes 147456 | tf_op jit(solution)/shard_map/all_gather | solution.py:222
  80.5 0.0 all-to-all-done
  80.5 4.2 %reshape.37 = bf16[2048,6,32]{2,1,0:T(8,128)(2,1)} reshape(bf16[8,2,24576]{2,1,0:T(2,128)(2,1)S(1)} %all-to-all-done) | data formatting | bytes 1572864
  84.6 4.2 %copy.29 = bf16[6,8,32,256]{3,2,1,0:T(8,128)(2,1)S(1)} copy(bf16[6,8,32,256]{2,0,3,1:T(8,128)(2,1)} %bitcast.57) | data formatting | bytes 1572864 | tf_op jit(solution)/shard_map/all_to_all | solution.py:227
  88.8 0.4 fusion
  89.2 1.0 copy.31
  90.2 33.0 %all_to_all.36 = bf16[6,256,256]{2,0,1:T(8,128)(2,1)S(1)} all-to-all(bf16[6,256,256]{2,0,1:T(8,128)(2,1)S(1)} %copy.31), channel_id=1, replica_groups=mesh['row'=8,'mem'=2,'lev'=2] {'row'}, dimensions={1} | all-to-all | bytes 1572864 | tf_op jit(solution)/shard_map/all_to_all | solution.py:230
  123.2 0.4 copy.33
  123.7 0.4 all_to_all.33
  124.0 0.1 collective-permute-start.1
  124.1 1.4 constant_dynamic-slice_fusion
  125.5 1.2 copy.44
  126.6 0.5 collective-permute-start
  127.1 0.2 copy.45
  127.3 0.0 collective-permute-done.1
  127.3 0.0 all-gather.2.cloned.1.call-done
  127.4 3.6 %fusion.8 = f32[192,1024]{1,0:T(8,128)S(1)} fusion(bf16[192,2048]{1,0:T(8,128)(2,1)} %bitcast.17, bf16[2048,1024]{1,0:T(8,128)(2,1)} %all-gather.2.cloned.1.call-done), kind=kOutput, calls=%fused_computation.19 | convolution fusion | flops 805306368 | bytes 5767168 | tf_op jit(solution)/shard_map/dot_general | solution.py:242
  130.9 0.1 fusion.6
  131.0 0.0 copy-done.3
  131.0 1.0 fusion.7
  132.1 0.1 fusion.5
  132.1 0.0 collective-permute-done
  132.2 0.5 copy-done.4
  132.7 1.9 %fusion.1.first = f32[3,3,32,1024]{3,2,1,0:T(8,128)S(1)} fusion(bf16[3,2,3,32,1024]{4,3,2,0,1:T(8,128)(2,1)} %collective-permute-done, bf16[3,2,3,32,2048]{4,3,2,1,0:T(8,128)(2,1)S(1)} %copy-done.4, s32[]{:T(128)S(6)} %add.28, s32[]{:T(128)S(6)} %select_n.9, f32[3,32,1024]{2,1,0:T(8,128)S(1)} %bitcast.64, f32[3,32,1024]{2,1,0:T(8,128)S(1)} %bitcast.63, ...), kind=kLoop, calls=%fused_computation.3 | loop fusion | flops 3244032 | bytes 5111816 | tf_op jit(solution)/shard_map/add | solution.py:248
  134.6 22.7 %advect.1 = f32[3,3,32,1024]{3,2,1,0:T(8,128)S(1)} custom-call(f32[3,3,32,1024]{3,2,1,0:T(8,128)S(1)} %fusion.1.first, f32[3,3,32,1024]{3,2,1,0:T(8,128)S(1)} %copy-done.1, f32[2,3,32,1024]{3,2,1,0:T(8,128)S(1)} %copy-done.2), custom_call_target="tpu_custom_call" | custom-call | tf_op jit(solution)/shard_map/advect/pallas_call | solution.py:189
  157.3 1.0 copy.47
  (12 shorter events, 0.0 us)
Async XLA Ops:
  6.5 1.2 copy-start
  6.5 2.1 %copy-start.5 = (bf16[2,3,32,2048]{3,2,1,0:T(8,128)(2,1)S(1)}, bf16[2,3,32,2048]{3,2,1,0:T(8,128)(2,1)}, u32[]{:S(2)}) copy-start(bf16[2,3,32,2048]{3,2,1,0:T(8,128)(2,1)} %param.6) | copy-start | bytes 2359300
  6.5 120.8 %all-gather.2.cloned.1.call-start = ((), (), s32[]{:S(2)}) async-start(), calls=%async_computation.2 | async-start | bytes 4718592 | tf_op jit(solution)/shard_map/all_gather | solution.py:221
  18.6 7.4 %copy-start.6 = (bf16[32,256]{1,0:T(8,128)(2,1)S(1)}, bf16[32,256]{1,0:T(8,128)(2,1)}, u32[]{:S(2)}) copy-start(bf16[32,256]{1,0:T(8,128)(2,1)} %param.9) | copy-start | bytes 49156
  18.6 61.9 %all-to-all-start = ((bf16[8,2,24576]{2,1,0:T(2,128)(2,1)}), bf16[8,2,24576]{2,1,0:T(2,128)(2,1)S(1)}, u32[]{:S(2)}, u32[]{:S(2)}) async-start(bf16[8,2,24576]{2,1,0:T(2,128)(2,1)} %reshape.36), calls=%async_computation | async-start | bytes 1572864 | tf_op jit(solution)/shard_map/all_to_all | solution.py:227
  124.0 3.3 %collective-permute-start.1 = (bf16[6,32,2048]{2,1,0:T(8,128)(2,1)S(1)}, bf16[6,32,2048]{2,1,0:T(8,128)(2,1)}, u32[]{:S(2)}, u32[]{:S(2)}) collective-permute-start(bf16[6,32,2048]{2,1,0:T(8,128)(2,1)S(1)} %all_to_all.33), channel_id=1, source_target_pairs={{0,2},{2,0},{1,3},{3,1},{4,6},{6,4},{5,7},{7,5},{8,10},{10,8},{9,1... | collective-permute-start | bytes 2359304 | tf_op jit(solution)/shard_map/ppermute | solution.py:241
  126.6 5.5 %collective-permute-start = (bf16[3,2,3,32,1024]{4,3,2,0,1:T(8,128)(2,1)}, bf16[3,2,3,32,1024]{4,3,2,0,1:T(8,128)(2,1)}, u32[]{:S(2)}, u32[]{:S(2)}) collective-permute-start(bf16[3,2,3,32,1024]{4,3,2,0,1:T(8,128)(2,1)} %copy.44), channel_id=1, source_target_pairs={{0,2},{2,0},{1,3},{3,1},{4,6},{6,4},{5,7},{7,5},{8,10},{10,8},{9,1... | collective-permute-start | bytes 3538952 | tf_op jit(solution)/shard_map/ppermute | solution.py:240
  127.4 3.7 %copy-start.3 = (bf16[2048,1024]{1,0:T(8,128)(2,1)S(1)}, bf16[2048,1024]{1,0:T(8,128)(2,1)}, u32[]{:S(2)}) copy-start(bf16[2048,1024]{1,0:T(8,128)(2,1)} %all-gather.2.cloned.1.call-done) | copy-start | bytes 12582916
  131.0 1.7 %copy-start.4 = (bf16[3,2,3,32,2048]{4,3,2,1,0:T(8,128)(2,1)S(1)}, bf16[3,2,3,32,2048]{4,3,2,1,0:T(8,128)(2,1)}, u32[]{:S(2)}) copy-start(bf16[3,2,3,32,2048]{4,3,2,1,0:T(8,128)(2,1)} %param.7) | copy-start | bytes 7077892
  132.7 1.9 %copy-start.1 = (f32[3,3,32,1024]{3,2,1,0:T(8,128)S(1)}, f32[3,3,32,1024]{3,2,1,0:T(8,128)}, u32[]{:S(2)}) copy-start(f32[3,3,32,1024]{3,2,1,0:T(8,128)} %courant.1) | copy-start | bytes 3538948
  132.7 1.9 %copy-start.2 = (f32[2,3,32,1024]{3,2,1,0:T(8,128)S(1)}, f32[2,3,32,1024]{3,2,1,0:T(8,128)}, u32[]{:S(2)}) copy-start(f32[2,3,32,1024]{3,2,1,0:T(8,128)} %slope.1) | copy-start | bytes 2359300
Sparse Core Ops, SparseCore 0:
  9.5 103.3 all-gather.1

commit v3 on v2

--- a/solution.py
+++ b/solution.py
@@ -209,43 +209,265 @@
     )(weighted, courant_numbers, tracer_slope)
 
 
+def localize_kernel(
+    control, pert, taper, row_part, out, gathered, row_all, staged, halves, taper_all, pert_all,
+    total, one_send, one_recv, row_send, row_recv, two_send, two_recv, pass_send, pass_recv,
+    pert_send, pert_recv, ring_send, ring_recv, lev_send, lev_recv, own_sem,
+):
+    count, mems, levs = (lax.axis_size(axis) for axis in ("row", "mem", "lev"))
+    me, mem_at, lev_at = (lax.axis_index(axis) for axis in ("row", "mem", "lev"))
+    fields, rows, depth = control.shape[1:]
+    kinds, members, levels = pert.shape[:3]
+    width = out.shape[3]
+    chains = ring_send.shape[0]
+    lanes, share = width // chains, depth // levs
+    half = count // 2
+
+    def order(place):
+        place = (place + 2 * count) % count
+        late = place // half
+        return (1 - late) * 2 * place + late * (2 * (count - 1 - place) + 1)
+
+    place = (1 - me % 2) * (me // 2) + (me % 2) * (count - 1 - me // 2)
+
+    def remote(source, landing, sent, landed, **target):
+        return pltpu.make_async_remote_copy(
+            src_ref=source, dst_ref=landing, send_sem=sent, recv_sem=landed,
+            device_id=target, device_id_type=MESH,
+        )
+
+    def own_columns(at):
+        return pl.ds(pl.multiple_of(at * width, width), width)
+
+    def one(peer, slot):
+        return remote(control.at[peer], gathered.at[slot], one_send.at[peer], one_recv.at[slot], row=peer)
+
+    def row(peer, slot):
+        return remote(row_part, row_all.at[slot], row_send.at[peer], row_recv.at[slot], row=peer)
+
+    def two(peer, slot):
+        return remote(
+            staged.at[peer], halves.at[mem_at, slot], two_send.at[peer], two_recv.at[slot], row=peer
+        )
+
+    def onward(peer, slot, place_of):
+        return remote(
+            halves.at[place_of, slot], halves.at[place_of, slot], pass_send.at[peer, slot],
+            pass_recv.at[place_of, slot], mem=peer,
+        )
+
+    def pert_copy(peer, slot):
+        return remote(
+            pert.at[:, :, :, :, own_columns(peer)], pert_all.at[slot], pert_send.at[peer],
+            pert_recv.at[slot], mem=peer,
+        )
+
+    def piece(chain, origin, lev):
+        return taper_all.at[
+            origin, pl.ds(pl.multiple_of(lev * share, share), share), pl.ds(chain * lanes, lanes)
+        ]
+
+    def ring(chain, hop, sending):
+        way = 1 - 2 * (chain % 2)
+        origin = order(place - way * hop) if sending else order(place - way * (hop + 1))
+        part = piece(chain, origin, lev_at)
+        return remote(part, part, ring_send.at[chain, hop], ring_recv.at[chain, hop], row=order(place + way))
+
+    def across(chain, hop, shift, sending):
+        way = 1 - 2 * (chain % 2)
+        origin = order(place - way * (hop + 1))
+        peer = (lev_at + shift) % levs
+        source = (lev_at + levs - shift) % levs
+        part = piece(chain, origin, lev_at if sending else source)
+        return remote(
+            part, part, lev_send.at[chain, hop, shift - 1], lev_recv.at[chain, hop, shift - 1], lev=peer
+        )
+
+    def ring_step(hop, last):
+        for chain in range(chains):
+            ring(chain, hop - 1, False).wait_recv()
+            if not last:
+                ring(chain, hop, True).start()
+            for shift in range(1, levs):
+                across(chain, hop - 1, shift, True).start()
+
+    barrier = pltpu.get_barrier_semaphore()
+    for axis, here, size in (("row", me, count), ("mem", mem_at, mems), ("lev", lev_at, levs)):
+
+        @pl.loop(1, size)
+        def _(shift):
+            pl.semaphore_signal(
+                barrier, inc=1, device_id={axis: (here + shift) % size}, device_id_type=MESH
+            )
+
+    own_taper = pltpu.make_async_copy(taper.at[:, own_columns(mem_at)], taper_all.at[me], own_sem.at[0])
+    own_taper.start()
+    own_pert = pltpu.make_async_copy(
+        pert.at[:, :, :, :, own_columns(mem_at)], pert_all.at[mem_at], own_sem.at[1]
+    )
+    own_pert.start()
+    gathered[me] = control[me]
+    row_all[me] = row_part[...]
+    own_taper.wait()
+    pl.semaphore_wait(barrier, count + mems + levs - 3)
+
+    @pl.loop(1, count)
+    def _(shift):
+        peer = (me + shift) % count
+        row(peer, me).start()
+        one(peer, me).start()
+
+    for chain in range(chains):
+        ring(chain, 0, True).start()
+
+    @pl.loop(1, mems)
+    def _(shift):
+        pert_copy((mem_at + shift) % mems, mem_at).start()
+
+    ring_step(1, count == 2)
+
+    @pl.loop(1, count)
+    def _(shift):
+        peer = (me + shift) % count
+        row(peer, peer).wait_recv()
+        one(peer, peer).wait_recv()
+
+    row_whole = row_all[...].reshape(count * rows, count * rows)
+
+    @pl.loop(0, fields)
+    def _(field):
+        tapered = jnp.dot(
+            row_whole,
+            gathered[:, field].reshape(count * rows, depth),
+            preferred_element_type=jnp.float32,
+        )
+        staged[:, field] = tapered.astype(jnp.bfloat16).reshape(count, rows, depth)
+
+    @pl.loop(1, count)
+    def _(shift):
+        two((me + shift) % count, me).start()
+
+    halves[mem_at, me] = staged[me]
+
+    @pl.loop(1, mems)
+    def _(shift):
+        onward((mem_at + shift) % mems, me, mem_at).start()
+
+    if count > 2:
+
+        @pl.loop(2, count - 1)
+        def _(hop):
+            ring_step(hop, False)
+
+        ring_step(count - 1, True)
+
+    @pl.loop(1, count)
+    def _(shift):
+        slot = (me + shift) % count
+        two(slot, slot).wait_recv()
+
+        @pl.loop(1, mems)
+        def _(step):
+            onward((mem_at + step) % mems, slot, mem_at).start()
+
+    @pl.loop(1, mems)
+    def _(step):
+        peer = (mem_at + step) % mems
+        pert_copy(peer, peer).wait_recv()
+
+        @pl.loop(0, count)
+        def _(slot):
+            onward(peer, slot, peer).wait_recv()
+
+    @pl.loop(0, count - 1)
+    def _(hop):
+        for chain in range(chains):
+            for shift in range(1, levs):
+                across(chain, hop, shift, False).wait_recv()
+
+    total[...] = jnp.zeros_like(total)
+
+    @pl.loop(0, count)
+    def _(slot):
+        total[...] += jnp.dot(
+            halves[:, slot].reshape(mems * fields * rows, depth),
+            taper_all[slot],
+            preferred_element_type=jnp.float32,
+        )
+
+    own_pert.wait()
+    for level in range(levels):
+        for kind in range(kinds):
+            weighted = jnp.zeros((rows, width), jnp.float32)
+            for mem in range(mems):
+                for member in range(members):
+                    at = ((mem * members + member) * levels + level) * rows
+                    weighted = weighted + pert_all[mem, kind, member, level].astype(
+                        jnp.float32
+                    ) * total[pl.ds(at, rows)]
+            out[kind, level] = weighted
+
+    @pl.loop(1, count)
+    def _(shift):
+        peer = (me + shift) % count
+        row(peer, me).wait_send()
+        one(peer, me).wait_send()
+        two(peer, me).wait_send()
+
+    @pl.loop(1, mems)
+    def _(shift):
+        peer = (mem_at + shift) % mems
+        pert_copy(peer, mem_at).wait_send()
+
+        @pl.loop(0, count)
+        def _(slot):
+            onward(peer, slot, mem_at).wait_send()
+
+    @pl.loop(0, count - 1)
+    def _(hop):
+        for chain in range(chains):
+            ring(chain, hop, True).wait_send()
+            for shift in range(1, levs):
+                across(chain, hop, shift, True).wait_send()
+
+
+def localized(control_fields, perturbations, column_taper, row_taper):
+    members, levels, rows, columns = control_fields.shape
+    kinds = perturbations.shape[0]
+    count, mems, levs = (lax.axis_size(axis) for axis in ("row", "mem", "lev"))
+    fields, depth, width = members * levels, columns // count, columns // mems
+    split = control_fields.reshape(fields, rows, count, depth).transpose(2, 0, 1, 3)
+    chains = 4 if width % 512 == 0 else 2
+    low, dma = jnp.bfloat16, pltpu.SemaphoreType.DMA
+    return pl.pallas_call(
+        localize_kernel,
+        out_shape=jax.ShapeDtypeStruct((kinds, levels, rows, width), jnp.float32),
+        in_specs=[pl.BlockSpec(memory_space=pltpu.VMEM)] * 4,
+        out_specs=pl.BlockSpec(memory_space=pltpu.VMEM),
+        scratch_shapes=[
+            pltpu.VMEM((count, fields, rows, depth), low),
+            pltpu.VMEM((count, rows, count * rows), low),
+            pltpu.VMEM((count, fields, rows, depth), low),
+            pltpu.VMEM((mems, count, fields, rows, depth), low),
+            pltpu.VMEM((count, depth, width), low),
+            pltpu.VMEM((mems, kinds, members, levels, rows, width), low),
+            pltpu.VMEM((mems * fields * rows, width), jnp.float32),
+            dma((count,)), dma((count,)), dma((count,)), dma((count,)), dma((count,)), dma((count,)),
+            dma((mems, count)), dma((mems, count)), dma((mems,)), dma((mems,)),
+            dma((chains, count)), dma((chains, count)),
+            dma((chains, count, levs)), dma((chains, count, levs)), dma((2,)),
+        ],
+        compiler_params=pltpu.CompilerParams(
+            collective_id=0, has_side_effects=True, vmem_limit_bytes=56 << 20
+        ),
+        name="localize",
+    )(split, perturbations, column_taper, row_taper)
+
+
 def on_device(
     control_fields, perturbations, column_taper, row_taper, courant_numbers, tracer_slope
 ):
-    member_count, level_count, row_count, column_count = control_fields.shape
-    field_count = member_count * level_count
-    mem_count = lax.axis_size("mem")
-    mem_at = lax.axis_index("mem")
-    width = column_count // mem_count
-    own_block = lax.dynamic_slice_in_dim(column_taper, mem_at * width, width, 1)
-    taper_columns = lax.all_gather(own_block, "row", axis=0, tiled=True)
-    row_whole = lax.all_gather(row_taper, "row", axis=0, tiled=True)
-    fields = control_fields.reshape(field_count, row_count, column_count)
-    tapered = jnp.einsum(
-        "ij,fjc->fic",
-        row_whole,
-        lax.all_to_all(fields, "row", split_axis=2, concat_axis=1, tiled=True),
-        preferred_element_type=jnp.float32,
-    )
-    tapered = lax.all_to_all(
-        tapered.astype(jnp.bfloat16), "row", split_axis=1, concat_axis=2, tiled=True
-    )
-    weighted = 0.0
-    for shift in range(mem_count):
-        ring = [(i, (i + shift) % mem_count) for i in range(mem_count)]
-        target = lax.rem(mem_at + shift, mem_count)
-        part = lax.dynamic_slice_in_dim(perturbations, target * width, width, 4)
-        half = tapered
-        if shift:
-            part = lax.ppermute(part, "mem", ring)
-            half = lax.ppermute(half, "mem", ring)
-        localized = jnp.dot(
-            half.reshape(field_count * row_count, column_count),
-            taper_columns,
-            preferred_element_type=jnp.float32,
-        ).reshape(member_count, level_count, row_count, width)
-        for m in range(member_count):
-            weighted = weighted + part[:, m].astype(jnp.float32) * localized[m][None]
+    weighted = localized(control_fields, perturbations, column_taper, row_taper)
     return advected(weighted, courant_numbers, tracer_slope)
 
 

time: 166 us -> 119 us (0.72)
  Pallas kernels: 22.7 us -> 113 us
  blocking collectives: 87.5 us -> 0 us
  local copies, waits for them, and re-layouts: 26.5 us -> 4.67 us
  between operations: 13.6 us -> 0.05 us
  starting transfers between devices: 7.97 us -> 0 us
  matrix products: 4.99 us -> 0 us
  other arithmetic: 1.92 us -> 0 us
    pallas_call x0 -> x1, Pallas kernels: none -> 88.1 us  [localized(): pl.pallas_call(localize_kernel, out_shape=jax.ShapeDtypeStruct((kinds, le...]
    all_gather x1 -> x0, blocking collectives: 54.5 us -> none  [on_device(): row_whole = lax.all_gather(row_taper, 'row', axis=0, tiled=True)]
    all_to_all x1 -> x0, blocking collectives: 33 us -> none  [on_device(): lax.all_to_all(tapered.astype(jnp.bfloat16), 'row', split_axis=1, concat_...]
    unnamed x19 -> x8, local copies, waits for them, and re-layouts: 14 us -> 3.61 us
    all_to_all x1 -> x0, starting transfers between devices: 7.41 us -> none  [on_device(): lax.all_to_all(fields, 'row', split_axis=2, concat_axis=1, tiled=True)]
    dot_general x3 -> x0, matrix products: 4.99 us -> none  [the longest x2 4.58 us: on_device(): jnp.dot(half.reshape(field_count * row_count, column_count), taper_column...]
    all_to_all x3 -> x0, local copies, waits for them, and re-layouts: 4.97 us -> none  [the longest x1 4.17 us: on_device(): lax.all_to_all(fields, 'row', split_axis=2, concat_axis=1, tiled=True)]
    reshape x1, local copies, waits for them, and re-layouts: 4.21 us -> 1.06 us  [localized(): control_fields.reshape(fields, rows, count, depth).transpose(2, 0, 1, 3)]
  transfers between devices with their start and end apart: 4 -> 0, of which waited for: 0 -> 0; matrix products, arithmetic and copies ran while one was open for 17% -> 0% of each run, Pallas kernels for 0% -> 0%
where the time goes in v3:
time: 119 us; the launch traced here: 117 us
  Pallas kernels  113 us (95%)
  local copies, waits for them, and re-layouts  4.67 us (4%)
    pallas_call x1, Pallas kernels, localized(): pl.pallas_call(localize_kernel, out_shape=jax.ShapeDtypeStruct((kinds, le...  88.1 us
    pallas_call x1, Pallas kernels, advected(): pl.pallas_call(advect_kernel, out_shape=jax.ShapeDtypeStruct(weighted.sha...  24.6 us
    unnamed x8, local copies, waits for them, and re-layouts  3.61 us

profile of v3, /device:TPU:0, one launch (start us, length us, event | category | flops | bytes accessed | tf_op | source)
XLA Modules:
  0.0 117.4 jit_solution(16674475259648189411)
XLA Ops:
  0.0 1.3 %copy.8 = bf16[24,8,8,256]{3,2,1,0:T(8,128)(2,1)S(1)} copy(bf16[24,8,8,256]{3,1,2,0:T(8,128)(2,1)} %bitcast.10) | data formatting | bytes 1572864
  1.3 1.1 copy.10
  2.4 0.0 copy-start.1
  2.4 0.0 copy-start.2
  2.4 88.1 %localize.1.first = f32[3,3,32,1024]{3,2,1,0:T(8,128)} custom-call(bf16[8,6,32,256]{3,2,1,0:T(8,128)(2,1)} %bitcast.9, bf16[3,2,3,32,2048]{4,3,2,1,0:T(8,128)(2,1)} %pert.1, bf16[256,2048]{1,0:T(8,128)(2,1)} %taper.1, bf16[32,256]{1,0:T(8,128)(2,1)} %row_part.1), custom_call_target="tpu_custom_call" | custom-call | tf_op jit(solution)/shard_map/localize/pallas_call | solution.py:442
  90.5 0.0 copy-done.1
  90.5 0.0 copy-done.2
  90.6 0.0 copy-start
  90.6 1.3 %copy-done = f32[3,3,32,1024]{3,2,1,0:T(8,128)S(1)} copy-done((f32[3,3,32,1024]{3,2,1,0:T(8,128)S(1)}, f32[3,3,32,1024]{3,2,1,0:T(8,128)}, u32[]{:S(2)}) %copy-start) | copy-done | bytes 1179672
  91.8 24.6 %advect.1 = f32[3,3,32,1024]{3,2,1,0:T(8,128)S(1)} custom-call(f32[3,3,32,1024]{3,2,1,0:T(8,128)S(1)} %copy-done, f32[3,3,32,1024]{3,2,1,0:T(8,128)S(1)} %copy-done.1, f32[2,3,32,1024]{3,2,1,0:T(8,128)S(1)} %copy-done.2), custom_call_target="tpu_custom_call" | custom-call | tf_op jit(solution)/shard_map/advect/pallas_call | solution.py:189
  116.4 1.0 copy.12
Async XLA Ops:
  2.4 88.1 %copy-start.1 = (f32[3,3,32,1024]{3,2,1,0:T(8,128)S(1)}, f32[3,3,32,1024]{3,2,1,0:T(8,128)}, u32[]{:S(2)}) copy-start(f32[3,3,32,1024]{3,2,1,0:T(8,128)} %courant.1) | copy-start | bytes 3538948
  2.4 88.1 %copy-start.2 = (f32[2,3,32,1024]{3,2,1,0:T(8,128)S(1)}, f32[2,3,32,1024]{3,2,1,0:T(8,128)}, u32[]{:S(2)}) copy-start(f32[2,3,32,1024]{3,2,1,0:T(8,128)} %slope.1) | copy-start | bytes 2359300
  90.6 1.3 %copy-start = (f32[3,3,32,1024]{3,2,1,0:T(8,128)S(1)}, f32[3,3,32,1024]{3,2,1,0:T(8,128)}, u32[]{:S(2)}) copy-start(f32[3,3,32,1024]{3,2,1,0:T(8,128)} %localize.1.first) | copy-start | bytes 3538948

commit v4 on v3

--- a/solution.py
+++ b/solution.py
@@ -311,20 +311,22 @@
     own_taper.wait()
     pl.semaphore_wait(barrier, count + mems + levs - 3)
 
+    for chain in range(chains):
+        ring(chain, 0, True).start()
+
     @pl.loop(1, count)
     def _(shift):
         peer = (me + shift) % count
         row(peer, me).start()
         one(peer, me).start()
 
-    for chain in range(chains):
-        ring(chain, 0, True).start()
-
     @pl.loop(1, mems)
     def _(shift):
         pert_copy((mem_at + shift) % mems, mem_at).start()
 
-    ring_step(1, count == 2)
+    early = max(1, min(3, count - 2))
+    for hop in range(1, early + 1):
+        ring_step(hop, count == 2)
 
     @pl.loop(1, count)
     def _(shift):
@@ -355,7 +357,7 @@
 
     if count > 2:
 
-        @pl.loop(2, count - 1)
+        @pl.loop(early + 1, count - 1)
         def _(hop):
             ring_step(hop, False)
 

time: 119 us -> 110 us (0.924); the launches traced: 117 us -> 110 us
  Pallas kernels: 113 us -> 105 us
    pallas_call x1, Pallas kernels: 88.1 us -> 80.2 us  [localized(): pl.pallas_call(localize_kernel, out_shape=jax.ShapeDtypeStruct((kinds, le...]
where the time goes in v4:
time: 110 us
  Pallas kernels  105 us (95%)
  local copies, waits for them, and re-layouts  4.67 us (4%)
    pallas_call x1, Pallas kernels, localized(): pl.pallas_call(localize_kernel, out_shape=jax.ShapeDtypeStruct((kinds, le...  80.2 us
    pallas_call x1, Pallas kernels, advected(): pl.pallas_call(advect_kernel, out_shape=jax.ShapeDtypeStruct(weighted.sha...  24.9 us
    unnamed x8, local copies, waits for them, and re-layouts  3.61 us

profile of v4, /device:TPU:0, one launch (start us, length us, event | category | flops | bytes accessed | tf_op | source)
XLA Modules:
  0.0 109.9 jit_solution(2928373905273837064)
XLA Ops:
  0.0 1.3 %copy.8 = bf16[24,8,8,256]{3,2,1,0:T(8,128)(2,1)S(1)} copy(bf16[24,8,8,256]{3,1,2,0:T(8,128)(2,1)} %bitcast.10) | data formatting | bytes 1572864
  1.3 1.1 copy.10
  2.4 0.0 copy-start.1
  2.4 0.0 copy-start.2
  2.4 80.2 %localize.1.first = f32[3,3,32,1024]{3,2,1,0:T(8,128)} custom-call(bf16[8,6,32,256]{3,2,1,0:T(8,128)(2,1)} %bitcast.9, bf16[3,2,3,32,2048]{4,3,2,1,0:T(8,128)(2,1)} %pert.1, bf16[256,2048]{1,0:T(8,128)(2,1)} %taper.1, bf16[32,256]{1,0:T(8,128)(2,1)} %row_part.1), custom_call_target="tpu_custom_call" | custom-call | tf_op jit(solution)/shard_map/localize/pallas_call | solution.py:444
  82.6 0.0 copy-done.1
  82.6 0.0 copy-done.2
  82.6 0.0 copy-start
  82.6 1.3 %copy-done = f32[3,3,32,1024]{3,2,1,0:T(8,128)S(1)} copy-done((f32[3,3,32,1024]{3,2,1,0:T(8,128)S(1)}, f32[3,3,32,1024]{3,2,1,0:T(8,128)}, u32[]{:S(2)}) %copy-start) | copy-done | bytes 1179672
  83.9 24.9 %advect.1 = f32[3,3,32,1024]{3,2,1,0:T(8,128)S(1)} custom-call(f32[3,3,32,1024]{3,2,1,0:T(8,128)S(1)} %copy-done, f32[3,3,32,1024]{3,2,1,0:T(8,128)S(1)} %copy-done.1, f32[2,3,32,1024]{3,2,1,0:T(8,128)S(1)} %copy-done.2), custom_call_target="tpu_custom_call" | custom-call | tf_op jit(solution)/shard_map/advect/pallas_call | solution.py:189
  108.9 1.0 copy.12
Async XLA Ops:
  2.4 80.2 %copy-start.1 = (f32[3,3,32,1024]{3,2,1,0:T(8,128)S(1)}, f32[3,3,32,1024]{3,2,1,0:T(8,128)}, u32[]{:S(2)}) copy-start(f32[3,3,32,1024]{3,2,1,0:T(8,128)} %courant.1) | copy-start | bytes 3538948
  2.4 80.2 %copy-start.2 = (f32[2,3,32,1024]{3,2,1,0:T(8,128)S(1)}, f32[2,3,32,1024]{3,2,1,0:T(8,128)}, u32[]{:S(2)}) copy-start(f32[2,3,32,1024]{3,2,1,0:T(8,128)} %slope.1) | copy-start | bytes 2359300
  82.6 1.3 %copy-start = (f32[3,3,32,1024]{3,2,1,0:T(8,128)S(1)}, f32[3,3,32,1024]{3,2,1,0:T(8,128)}, u32[]{:S(2)}) copy-start(f32[3,3,32,1024]{3,2,1,0:T(8,128)} %localize.1.first) | copy-start | bytes 3538948
